TPU v7x, 128 devices: a whole 4x4x4 slice. The times are simulated.
128 devices in a mesh: group: 16 (over x, z_lo, core), head: 8 (over y, z_hi).
Axes of the slice: x: 4, y: 4, z: 4 (z_hi: 2, z_lo: 2; z = z_hi * 2 + z_lo), core: 2. Of those that a mesh axis runs over, the one named last changes fastest.
Arguments:
- hidden_in: bfloat16 [256, 2560], P('group'), may hold values from -6 to 6
- ssm_state: float32 [256, 80, 64, 128], P('group', 'head'), may hold values from -6 to 6
- conv_x_state: bfloat16 [256, 3, 5120], P('group', None, 'head'), may hold values from -6 to 6
- conv_bc_state: bfloat16 [256, 3, 256], P('group'), may hold values from -6 to 6
- token_ids: int32 [256], P('group'), may hold values from 0 to 25599
- ref_logits: bfloat16 [256, 25600], P('group', 'head'), may hold values from -15 to 350
- in_z: bfloat16 [2560, 5120], P('group', 'head'), may hold values from -0.125 to 0.125
- in_x: bfloat16 [2560, 5120], P('group', 'head'), may hold values from -0.125 to 0.125
- in_bc: bfloat16 [2560, 256], P('group'), may hold values from -0.125 to 0.125
- in_dt: bfloat16 [2560, 80], P('group', 'head'), may hold values from -0.125 to 0.125
- out_t: bfloat16 [2560, 5120], P('group', 'head'), may hold values from -0.078125 to 0.078125
- lm_head: bfloat16 [25600, 2560], P('head', 'group'), may hold values from -6 to 6
- conv_wx: float32 [4, 5120], P(None, 'head'), may hold values from -3 to 3
- conv_bx: float32 [5120], P('head'), may hold values from -1.5 to 1.5
- conv_wbc: float32 [4, 256], replicated, may hold values from -3 to 3
- conv_bbc: float32 [256], replicated, may hold values from -1.5 to 1.5
- dt_bias: float32 [80], P('head'), may hold values from -4 to -1
- a_log: float32 [80], P('head'), may hold values from 0 to 2.77
- skip_gain: float32 [80], P('head'), may hold values from 0.5 to 1.5
- norm_in: float32 [2560], replicated, may hold values from 0.5 to 1.5
- norm_gain: float32 [5120], P('head'), may hold values from 0.5 to 1.5
- final_gain: float32 [2560], replicated, may hold values from 0.5 to 1.5
Outputs:
- new_state: float32 [256, 80, 64, 128], P('group', 'head')
- divergence: float32 [256], P('group')
- token_logprob: float32 [256], P('group')
- roll_z: bfloat16 [2560, 5120], P(None, 'head')
- roll_x: bfloat16 [2560, 5120], P(None, 'head')
- roll_bc: bfloat16 [2560, 256], replicated
- roll_dt: bfloat16 [2560, 80], P(None, 'head')
- roll_out: bfloat16 [2560, 5120], P(None, 'head')
All inputs are finite; a program needn't handle non-finite values.
Results may differ from a plain program's by a relative error of at most 0.0102.
Values may be sent and summed in bfloat16 or wider, within the bound.
A program may use at most 128 MiB of HBM per device.

v0:
```python
import functools

import jax
import jax.numpy as jnp
from jax import lax
from jax.experimental import pallas as pl
from jax.experimental.pallas import tpu as pltpu
from jax.sharding import PartitionSpec as P

MESH = pl.DeviceIdType.MESH
EPSILON = 1e-05
SEQS, D, DI, HEADS, P_SIZE, N = 16, 2560, 640, 10, 64, 128
SHARD = 160
SLICE = 320
CHIPS = 8
VL = 3200
F32 = jnp.float32
BF16 = jnp.bfloat16

PIECES = {
    "X": ("x", 0, 160, False),
    "OL": ("o", 0, 80, False),
    "DT": ("d", 0, 160, False),
    "Z": ("z", 0, 160, True),
    "BC": ("b", 0, 160, True),
    "OH": ("o", 80, 80, True),
}
ORDER = {name: at for at, name in enumerate(PIECES)}


def silu(v):
    return v / (1.0 + jnp.exp(-v))


def per_head(values):
    rows = values.shape[0]
    lane = lax.broadcasted_iota(jnp.int32, (rows, 128), 1)
    parts = []
    for pair in range(HEADS // 2):
        left = jnp.broadcast_to(values[:, 2 * pair : 2 * pair + 1], (rows, 128))
        right = jnp.broadcast_to(values[:, 2 * pair + 1 : 2 * pair + 2], (rows, 128))
        parts.append(jnp.where(lane < P_SIZE, left, right))
    return jnp.concatenate(parts, axis=1)


def as_column(row):
    r = lax.broadcasted_iota(jnp.int32, (SEQS, SEQS), 0)
    c = lax.broadcasted_iota(jnp.int32, (SEQS, SEQS), 1)
    return jnp.sum(jnp.where(r == c, jnp.broadcast_to(row, (SEQS, SEQS)), 0.0), axis=1, keepdims=True)


def as_row(column):
    r = lax.broadcasted_iota(jnp.int32, (SEQS, 128), 0)
    c = lax.broadcasted_iota(jnp.int32, (SEQS, 128), 1)
    return jnp.sum(jnp.where(r == c, jnp.broadcast_to(column, (SEQS, 128)), 0.0), axis=0, keepdims=True)


def two_parts(values, width):
    high = values.astype(BF16)
    low = (values - high.astype(F32)).astype(BF16)
    rows = values.shape[0]
    return jnp.concatenate(
        [jnp.broadcast_to(high.astype(F32), (rows, width)), jnp.broadcast_to(low.astype(F32), (rows, width))], axis=1
    )


def kernel(
    hidden_in, state_in, conv_x_in, conv_bc_in, tokens_in, ref_in, in_z, in_x, in_bc, dt_in, out_t, lm_in,
    conv_wx_in, conv_bx, conv_wbc_in, conv_bbc_in, dt_bias_in, a_log_in, skip_in, norm_in, norm_gain, final_gain,
    state, div_out, logprob_out, zg, xg, bg, dt_out, og,
    dg, lm, refs, hsend, hrecv, gains, psend, precv, gsend, grecv, rsend, rrecv, usend, urecv, lsend, lrecv,
    ssend, srecv, decays, b_parts, x_cols, c_rows, y_acc,
    hidden, conv_x, conv_bc, tokens, in_dt, conv_wx, conv_wbc, conv_bbc, dt_bias, a_log, skip_gain,
    long_rows, short_rows, loc, small, chain_s, chain_r, ag_s, ag_r, d2_s, d2_r,
):
    g = lax.axis_index("group")
    h = lax.axis_index("head")
    k = g // 2
    c = g % 2
    x = k // 2
    zl = k % 2
    sibling = (2 * k + 1 - c, h)

    barrier = pltpu.get_barrier_semaphore()
    pl.semaphore_signal(barrier, inc=1, device_id=sibling, device_id_type=MESH)
    for d in range(1, 8):
        pl.semaphore_signal(barrier, inc=1, device_id=(2 * ((k + d) % 8) + c, h), device_id_type=MESH)
        pl.semaphore_signal(barrier, inc=1, device_id=(g, (h + d) % 8), device_id_type=MESH)

    rows_mine = pl.ds(pl.multiple_of(g * SHARD, SHARD), SHARD)
    lm_rows = pl.ds(pl.multiple_of(c * SHARD, SHARD), SHARD)
    local = [
        pltpu.make_async_copy(source, target, loc.at[at])
        for at, (source, target) in enumerate(
            [
                (in_x, xg.at[rows_mine]), (in_bc, bg.at[rows_mine]), (in_z, zg.at[rows_mine]),
                (out_t, og.at[rows_mine]), (lm_in, lm.at[lm_rows]), (state_in, state), (ref_in, refs),
                (norm_in, long_rows.at[0]), (final_gain, long_rows.at[1]), (conv_bx, short_rows.at[0]),
                (norm_gain, short_rows.at[1]),
            ]
        )
    ]
    first = [
        pltpu.make_async_copy(source, target, small.at[at])
        for at, (source, target) in enumerate(
            [
                (hidden_in, hidden), (dt_in, in_dt), (conv_x_in, conv_x), (conv_bc_in, conv_bc), (tokens_in, tokens),
                (conv_wx_in, conv_wx), (conv_wbc_in, conv_wbc), (conv_bbc_in, conv_bbc), (dt_bias_in, dt_bias),
                (a_log_in, a_log), (skip_in, skip_gain),
            ]
        )
    ]
    for copy in first + local:
        copy.start()
    first[0].wait()
    first[1].wait()

    for j in range(CHIPS):
        hsend[j] = hidden[:, SLICE * j : SLICE * (j + 1)]
    turned = jnp.transpose(jnp.concatenate([in_dt[...].astype(F32), jnp.zeros((128 - HEADS, SHARD), F32)], axis=0))
    dg[rows_mine, :] = turned.astype(BF16)
    local[7].wait()
    local[8].wait()
    for j in range(CHIPS):
        gains[0, j] = long_rows[0:1, SLICE * j : SLICE * (j + 1)]
        gains[1, j] = long_rows[1:2, SLICE * j : SLICE * (j + 1)]
    whole = hidden[...].astype(F32)
    scale_in = lax.rsqrt(jnp.mean(whole * whole, axis=-1, keepdims=True) + EPSILON)

    pl.semaphore_wait(barrier, 15)

    pending = []

    def chain_copy(phase, d, src, dst, device):
        return pltpu.make_async_remote_copy(
            src_ref=src, dst_ref=dst, send_sem=chain_s.at[phase, d], recv_sem=chain_r.at[phase, d],
            device_id=device, device_id_type=MESH,
        )

    def to_chips(phase, send_slot, recv):
        for d in range(1, 8):
            j = (k + d) % 8
            copy = chain_copy(phase, d, send_slot(j), recv.at[k], (2 * j + c, h))
            copy.start()
            pending.append(copy)

    def from_chips(phase, recv):
        for d in range(1, 8):
            j = (k + 8 - d) % 8
            chain_copy(phase, d, recv.at[j], recv.at[j], (2 * j + c, h)).wait_recv()

    def to_heads(phase, send_slot, recv):
        for d in range(1, 8):
            j = (h + d) % 8
            copy = chain_copy(phase, d, send_slot(j), recv.at[h], (g, j))
            copy.start()
            pending.append(copy)

    def from_heads(phase, recv):
        for d in range(1, 8):
            j = (h + 8 - d) % 8
            chain_copy(phase, d, recv.at[j], recv.at[j], (g, j)).wait_recv()

    buffers = {"x": xg, "z": zg, "o": og, "b": bg, "d": dg}

    def region(piece, dx, dz, core):
        name, first, rows, _ = PIECES[piece]
        at = ((((x + dx) % 4) * 2 + (zl + dz) % 2) * 2 + core) * SHARD + first
        return buffers[name].at[pl.ds(pl.multiple_of(at, 16), rows)]

    count = [0]

    def ici(piece, dx, dz, way):
        move = {"+": 1, "-": 3, "z": 0}[way]
        rx, rz = (dx - move) % 4, (dz + (way == "z")) % 2
        chip = ((x + move) % 4) * 2 + (zl + (way == "z")) % 2
        block = region(piece, dx, dz, c)
        copy = pltpu.make_async_remote_copy(
            src_ref=block, dst_ref=block, send_sem=ag_s.at[count[0]], recv_sem=ag_r.at[ORDER[piece], rx, rz],
            device_id=(2 * chip + c, h), device_id_type=MESH,
        )
        count[0] += 1
        copy.start()
        pending.append(copy)

    def on_chip(piece, dx, dz):
        block = region(piece, dx, dz, c)
        copy = pltpu.make_async_remote_copy(
            src_ref=block, dst_ref=block, send_sem=d2_s.at[ORDER[piece], dx, dz], recv_sem=d2_r.at[ORDER[piece], dx, dz],
            device_id=sibling, device_id_type=MESH,
        )
        copy.start()
        pending.append(copy)

    waited = set()

    def arrived(piece, dx, dz):
        block = region(piece, dx, dz, c)
        pltpu.make_async_remote_copy(
            src_ref=block, dst_ref=block, send_sem=d2_s.at[ORDER[piece], dx, dz], recv_sem=ag_r.at[ORDER[piece], dx, dz],
            device_id=sibling, device_id_type=MESH,
        ).wait_recv()
        waited.add((piece, dx, dz))
        on_chip(piece, dx, dz)

    chip_waited = set()

    def from_sibling(piece, dx, dz):
        block = region(piece, dx, dz, 1 - c)
        pltpu.make_async_remote_copy(
            src_ref=block, dst_ref=block, send_sem=d2_s.at[ORDER[piece], dx, dz], recv_sem=d2_r.at[ORDER[piece], dx, dz],
            device_id=sibling, device_id_type=MESH,
        ).wait_recv()
        chip_waited.add((piece, dx, dz))

    to_chips(0, lambda j: hsend.at[j], hrecv)
    hrecv[k] = hsend[k]
    local[0].wait()
    on_chip("X", 0, 0)
    local[1].wait()
    on_chip("BC", 0, 0)
    on_chip("DT", 0, 0)
    local[2].wait()
    on_chip("Z", 0, 0)
    ici("X", 0, 0, "+")
    ici("X", 0, 0, "-")
    ici("Z", 0, 0, "z")
    local[3].wait()
    on_chip("OL", 0, 0)
    on_chip("OH", 0, 0)
    local[4].wait()
    lm_copy = pltpu.make_async_remote_copy(
        src_ref=lm.at[lm_rows], dst_ref=lm.at[lm_rows], send_sem=loc.at[12], recv_sem=loc.at[13],
        device_id=sibling, device_id_type=MESH,
    )
    lm_copy.start()
    pending.append(lm_copy)

    from_chips(0, hrecv)
    gain = gains[0, k]
    lhs = (hrecv[...].astype(F32) * gain[None]).astype(BF16).reshape(CHIPS * SEQS, SLICE)
    slice_rows = pl.ds(pl.multiple_of(k * SLICE, SLICE), SLICE)

    def partial(weights, at, width):
        product = jnp.dot(lhs, weights[slice_rows, :], preferred_element_type=F32)
        psend[:, :, at : at + width] = product.astype(BF16).reshape(CHIPS, SEQS, width)

    from_sibling("X", 0, 0)
    partial(xg, 0, 640)
    from_sibling("BC", 0, 0)
    partial(bg, 640, 256)
    from_sibling("DT", 0, 0)
    partial(dg, 896, 128)
    to_chips(1, lambda j: psend.at[j, :, pl.ds(0, 1024)], precv.at[:, :, pl.ds(0, 1024)])
    from_sibling("Z", 0, 0)
    partial(zg, 1024, 640)
    to_chips(2, lambda j: psend.at[j, :, pl.ds(1024, 640)], precv.at[:, :, pl.ds(1024, 640)])
    precv[k] = psend[k]
    arrived("Z", 0, 1)
    ici("Z", 0, 0, "+")
    ici("Z", 0, 0, "-")
    ici("X", 0, 0, "z")

    for copy in first[2:] + local[9:]:
        copy.wait()
    from_chips(1, precv.at[:, :, pl.ds(0, 1024)])
    summed = jnp.sum(precv[:, :, 0:1024].astype(F32), axis=0) * scale_in
    x_new = summed[:, 0:640]
    bc_new = summed[:, 640:896]
    step_raw = summed[:, 896 : 896 + HEADS]
    acc = x_new * conv_wx[3:4, :] + short_rows[0:1, :]
    acc_bc = bc_new * conv_wbc[3:4, :] + conv_bbc[...]
    for tap in range(3):
        acc = acc + conv_x[tap].astype(F32) * conv_wx[tap : tap + 1, :]
        acc_bc = acc_bc + conv_bc[tap].astype(F32) * conv_wbc[tap : tap + 1, :]
    x_conv = silu(acc)
    bc_conv = silu(acc_bc)
    b_vals = bc_conv[:, :N]
    c_vals = bc_conv[:, N:]
    biased = step_raw + dt_bias[...]
    step = jnp.maximum(biased, 0.0) + jnp.log1p(jnp.exp(-jnp.abs(biased)))
    decays[:, 0:HEADS] = jnp.exp(-step * jnp.exp(a_log[...]))
    inflow = per_head(step) * x_conv
    in_high = inflow.astype(BF16).astype(F32)
    in_low = inflow - in_high
    stacked = jnp.concatenate([in_high, in_low, in_high, jnp.zeros_like(in_high)], axis=0)
    x_cols[...] = jnp.transpose(jnp.concatenate([stacked, jnp.zeros_like(stacked)], axis=0)).astype(BF16)
    b_high = b_vals.astype(BF16).astype(F32)
    b_low = b_vals - b_high
    b_parts[...] = jnp.concatenate([b_high, b_high, b_low, jnp.zeros((5 * SEQS, N), F32)], axis=0)
    c_high = c_vals.astype(BF16)
    c_low = (c_vals - c_high.astype(F32)).astype(BF16)
    c_rows[...] = jnp.concatenate([c_high, c_low], axis=0)
    y_acc[...] = jnp.zeros_like(y_acc)
    local[5].wait()

    def one_sequence(s, _):
        row = lax.broadcasted_iota(jnp.int32, (8 * SEQS, N), 0)
        picked_b = jnp.where(row % SEQS == s, b_parts[...], 0.0).astype(BF16)
        added = jnp.dot(x_cols[...], picked_b, preferred_element_type=F32)
        decay_row = decays[pl.ds(s, 1), :]
        for head in range(HEADS):
            rows = slice(head * P_SIZE, (head + 1) * P_SIZE)
            factor = jnp.broadcast_to(decay_row[:, head : head + 1], (P_SIZE, N))
            state[s, rows] = state[s, rows] * factor + added[rows]
        seen = lax.dot_general(
            c_rows[...], state[s].astype(BF16), (((1,), (1,)), ((), ())), preferred_element_type=F32
        )
        seen = seen[0:SEQS] + seen[SEQS:]
        which = lax.broadcasted_iota(jnp.int32, (SEQS, DI), 0)
        y_acc[...] += jnp.where(which == s, seen, 0.0)
        return 0

    lax.fori_loop(0, SEQS, one_sequence, 0)
    from_chips(2, precv.at[:, :, pl.ds(1024, 640)])
    gate = jnp.sum(precv[:, :, 1024:1664].astype(F32), axis=0) * scale_in
    ssm_out = y_acc[...] + per_head(skip_gain[...]) * x_conv
    gated = ssm_out * silu(gate)
    squares = jnp.sum(gated * gated, axis=-1, keepdims=True)
    gsend[:, 0:640] = (gated * short_rows[1:2, :]).astype(BF16)
    gsend[:, 640:768] = two_parts(squares, 64).astype(BF16)

    to_chips(3, lambda j: gsend, grecv)
    grecv[k] = gsend[...]
    arrived("X", 3, 0)
    ici("X", 3, 0, "+")
    ici("X", 3, 0, "z")
    arrived("X", 1, 0)
    ici("X", 1, 0, "z")
    ici("Z", 0, 1, "+")
    ici("Z", 0, 1, "-")
    ici("OL", 0, 0, "+")
    ici("OL", 0, 0, "-")

    from_sibling("OL", 0, 0)
    from_sibling("OH", 0, 0)
    from_chips(3, grecv)
    mixed = lax.dot_general(
        grecv[:, :, 0:640].reshape(CHIPS * SEQS, 640), og[slice_rows, :], (((1,), (1,)), ((), ())),
        preferred_element_type=F32,
    )
    parts = grecv[:, :, 640:768].astype(F32)
    sq = (parts[:, :, 0:1] + parts[:, :, 64:65])
    rsend[:, :, 0:SLICE] = mixed.reshape(CHIPS, SEQS, SLICE)
    rsend[:, :, 384:512] = jnp.broadcast_to(sq, (CHIPS, SEQS, 128))
    to_heads(4, lambda j: rsend.at[j], rrecv)
    rrecv[h] = rsend[h]
    ici("BC", 0, 0, "z")
    ici("OH", 0, 0, "z")
    ici("DT", 0, 0, "z")
    ici("OL", 0, 0, "z")
    from_heads(4, rrecv)
    total = jnp.sum(rrecv[...], axis=0)
    scale_gate = lax.rsqrt(total[:, 384:385] / (8.0 * DI) + EPSILON)
    stream = hrecv[h].astype(F32) + total[:, 0:SLICE] * scale_gate
    usend[:, 0:SLICE] = (stream * gains[1, k]).astype(BF16)
    usend[:, 384:512] = two_parts(jnp.sum(stream * stream, axis=-1, keepdims=True), 64).astype(BF16)

    to_heads(5, lambda j: usend, urecv)
    urecv[h] = usend[...]

    local[6].wait()
    pltpu.make_async_remote_copy(
        src_ref=lm.at[pl.ds(pl.multiple_of((1 - c) * SHARD, SHARD), SHARD)],
        dst_ref=lm.at[pl.ds(pl.multiple_of((1 - c) * SHARD, SHARD), SHARD)], send_sem=loc.at[12], recv_sem=loc.at[13],
        device_id=sibling, device_id_type=MESH,
    ).wait_recv()
    from_heads(5, urecv)
    final = urecv[:, :, 0:SLICE].reshape(CHIPS * SEQS, SLICE)

    def some_logits(block, _):
        at = pl.ds(pl.multiple_of(block * 640, 640), 640)
        product = jnp.dot(final, lm[:, at], preferred_element_type=F32)
        lsend[:, :, at] = product.astype(BF16).reshape(CHIPS, SEQS, 640)
        return 0

    lax.fori_loop(0, VL // 640, some_logits, 0)
    lsend[:, :, VL : VL + 128] = urecv[:, :, 384:512]
    to_chips(6, lambda j: lsend.at[j], lrecv)
    lrecv[k] = lsend[k]

    for way in "+-":
        ici("BC", 0, 0, way)
        ici("OH", 0, 0, way)
        ici("DT", 0, 0, way)
    arrived("X", 2, 0)
    ici("X", 2, 0, "z")
    arrived("Z", 3, 0)
    ici("Z", 3, 0, "+")
    arrived("Z", 1, 1)
    ici("Z", 1, 1, "-")
    arrived("OL", 1, 0)
    ici("OL", 1, 0, "-")
    ici("OL", 1, 0, "z")
    arrived("OL", 3, 0)
    ici("OL", 3, 0, "z")
    arrived("BC", 0, 1)
    arrived("OH", 0, 1)
    for way in "+-":
        ici("BC", 0, 1, way)
        ici("OH", 0, 1, way)

    reference = refs[...].astype(F32)
    ref_max = jnp.max(reference, axis=-1, keepdims=True)
    weight = jnp.exp(reference - ref_max)
    ref_sum = jnp.sum(weight, axis=-1, keepdims=True)

    arrived("DT", 1, 0)
    ici("DT", 1, 0, "-")
    ici("DT", 1, 0, "z")
    arrived("DT", 3, 0)
    ici("DT", 3, 0, "z")
    from_chips(6, lrecv)
    logits = jnp.sum(lrecv[:, :, 0:VL].astype(F32), axis=0)
    tail = jnp.sum(lrecv[:, :, VL : VL + 128].astype(F32), axis=0)
    logits = logits * lax.rsqrt((tail[:, 0:1] + tail[:, 64:65]) / D + EPSILON)
    roll_max = jnp.max(logits, axis=-1, keepdims=True)
    roll_sum = jnp.sum(jnp.exp(logits - roll_max), axis=-1, keepdims=True)
    cross = jnp.sum(weight * (reference - logits), axis=-1, keepdims=True)
    token = as_column(tokens[...].astype(F32)).astype(jnp.int32)
    column = lax.broadcasted_iota(jnp.int32, (SEQS, VL), 1) + h * VL
    picked = jnp.sum(jnp.where(column == token, logits, 0.0), axis=-1, keepdims=True)
    lane = lax.broadcasted_iota(jnp.int32, (SEQS, 128), 1)
    packed = jnp.zeros((SEQS, 128), F32)
    for at, value in enumerate((roll_max, roll_sum, ref_max, ref_sum, cross, picked)):
        packed = jnp.where(lane == at, jnp.broadcast_to(value, (SEQS, 128)), packed)
    ssend[...] = packed

    to_heads(7, lambda j: ssend, srecv)
    srecv[h] = ssend[...]

    arrived("BC", 3, 0)
    ici("BC", 3, 0, "+")
    arrived("OH", 3, 0)
    ici("OH", 3, 0, "+")
    arrived("BC", 1, 1)
    ici("BC", 1, 1, "-")
    arrived("OH", 1, 1)
    ici("OH", 1, 1, "-")
    arrived("OL", 2, 0)
    ici("OL", 2, 0, "z")
    arrived("DT", 2, 0)
    ici("DT", 2, 0, "z")

    from_heads(7, srecv)
    every = srecv[...]
    m_all, s_all, rm_all, rs_all, x_all, p_all = (every[:, :, at : at + 1] for at in range(6))
    roll_top = jnp.max(m_all, axis=0)
    roll_total = jnp.sum(s_all * jnp.exp(m_all - roll_top[None]), axis=0)
    ref_top = jnp.max(rm_all, axis=0)
    ref_scale = jnp.exp(rm_all - ref_top[None])
    ref_total = jnp.sum(rs_all * ref_scale, axis=0)
    cross_total = jnp.sum(x_all * ref_scale, axis=0)
    lse_roll = roll_top + jnp.log(roll_total)
    lse_ref = ref_top + jnp.log(ref_total)
    divergence = cross_total / ref_total - lse_ref + lse_roll
    logprob = jnp.sum(p_all, axis=0) - lse_roll
    div_out[...] = as_row(divergence)[:, 0:SEQS]
    logprob_out[...] = as_row(logprob)[:, 0:SEQS]

    for piece in PIECES:
        for dz in range(2):
            for dx in range(4):
                if (dx, dz) != (0, 0) and (piece, dx, dz) not in waited:
                    arrived(piece, dx, dz)
    for piece in PIECES:
        for dz in range(2):
            for dx in range(4):
                if (piece, dx, dz) not in chip_waited:
                    from_sibling(piece, dx, dz)
    for block in range(2):
        turned = jnp.transpose(dg[block * 1280 : (block + 1) * 1280, :].astype(F32))
        dt_out[:, block * 1280 : (block + 1) * 1280] = turned[0:HEADS].astype(BF16)
    for copy in pending:
        copy.wait_send()


def write_out(*refs):
    count = len(refs) // 2
    copies = [pltpu.make_async_copy(refs[at], refs[count + at], refs[-1].at[at]) for at in range(count)]
    for copy in copies:
        copy.start()
    for copy in copies:
        copy.wait()


ANY = pl.BlockSpec(memory_space=pl.ANY)
VMEM = pl.BlockSpec(memory_space=pltpu.VMEM)
SENDS = 64


def shards(
    hidden_in, ssm_state, conv_x_state, conv_bc_state, token_ids, ref_logits, in_z, in_x, in_bc, in_dt, out_t,
    lm_head, conv_wx, conv_bx, conv_wbc, conv_bbc, dt_bias, a_log, skip_gain, norm_in, norm_gain, final_gain,
):
    row = lambda v: v.reshape(1, -1)
    results = (
        ((SEQS, DI, N), F32), ((1, SEQS), F32), ((1, SEQS), F32), ((D, DI), BF16), ((D, DI), BF16), ((D, 256), BF16),
        ((HEADS, D), BF16), ((D, DI), BF16),
    )
    held = pl.pallas_call(
        kernel,
        out_shape=tuple(pltpu.VMEM(shape, dtype) for shape, dtype in results),
        in_specs=[pl.BlockSpec(memory_space=pltpu.HBM)] * 22,
        out_specs=(VMEM,) * len(results),
        scratch_shapes=[
            pltpu.VMEM((D, 128), BF16),
            pltpu.VMEM((SLICE, VL), BF16),
            pltpu.VMEM((SEQS, VL), BF16),
            pltpu.VMEM((CHIPS, SEQS, SLICE), BF16),
            pltpu.VMEM((CHIPS, SEQS, SLICE), BF16),
            pltpu.VMEM((2, CHIPS, 1, SLICE), F32),
            pltpu.VMEM((CHIPS, SEQS, 1664), BF16),
            pltpu.VMEM((CHIPS, SEQS, 1664), BF16),
            pltpu.VMEM((SEQS, 768), BF16),
            pltpu.VMEM((CHIPS, SEQS, 768), BF16),
            pltpu.VMEM((CHIPS, SEQS, 512), F32),
            pltpu.VMEM((CHIPS, SEQS, 512), F32),
            pltpu.VMEM((SEQS, 512), BF16),
            pltpu.VMEM((CHIPS, SEQS, 512), BF16),
            pltpu.VMEM((CHIPS, SEQS, VL + 128), BF16),
            pltpu.VMEM((CHIPS, SEQS, VL + 128), BF16),
            pltpu.VMEM((SEQS, 128), F32),
            pltpu.VMEM((CHIPS, SEQS, 128), F32),
            pltpu.VMEM((SEQS, 128), F32),
            pltpu.VMEM((8 * SEQS, N), F32),
            pltpu.VMEM((DI, 8 * SEQS), BF16),
            pltpu.VMEM((2 * SEQS, N), BF16),
            pltpu.VMEM((SEQS, DI), F32),
            pltpu.VMEM((SEQS, D), BF16),
            pltpu.VMEM((3, SEQS, DI), BF16),
            pltpu.VMEM((3, SEQS, 256), BF16),
            pltpu.VMEM((1, SEQS), jnp.int32),
            pltpu.VMEM((HEADS, SHARD), BF16),
            pltpu.VMEM((4, DI), F32),
            pltpu.VMEM((4, 256), F32),
            pltpu.VMEM((1, 256), F32),
            pltpu.VMEM((1, HEADS), F32),
            pltpu.VMEM((1, HEADS), F32),
            pltpu.VMEM((1, HEADS), F32),
            pltpu.VMEM((2, D), F32),
            pltpu.VMEM((2, DI), F32),
            pltpu.SemaphoreType.DMA((14,)),
            pltpu.SemaphoreType.DMA((11,)),
            pltpu.SemaphoreType.DMA((8, 8)),
            pltpu.SemaphoreType.DMA((8, 8)),
            pltpu.SemaphoreType.DMA((SENDS,)),
            pltpu.SemaphoreType.DMA((6, 4, 2)),
            pltpu.SemaphoreType.DMA((6, 4, 2)),
            pltpu.SemaphoreType.DMA((6, 4, 2)),
        ],
        compiler_params=pltpu.CompilerParams(
            collective_id=0, has_side_effects=True, vmem_limit_bytes=32 * 1024 * 1024
        ),
    )(*[pltpu.with_memory_space_constraint(array, pltpu.HBM) for array in (
        hidden_in, ssm_state.reshape(SEQS, DI, N), conv_x_state.transpose(1, 0, 2), conv_bc_state.transpose(1, 0, 2),
        row(token_ids), ref_logits, in_z, in_x, in_bc, in_dt.T, out_t, lm_head.T,
        conv_wx, conv_bx, conv_wbc, row(conv_bbc), row(dt_bias), row(a_log), row(skip_gain), norm_in,
        norm_gain, final_gain,
    )])
    held = [pltpu.with_memory_space_constraint(array, pltpu.VMEM) for array in held]
    state, divergence, logprob, roll_z, roll_x, roll_bc, dt_rows, roll_out = pl.pallas_call(
        write_out,
        out_shape=tuple(jax.ShapeDtypeStruct(shape, dtype) for shape, dtype in results),
        in_specs=[VMEM] * len(results),
        out_specs=(ANY,) * len(results),
        scratch_shapes=[pltpu.SemaphoreType.DMA((len(results),))],
        compiler_params=pltpu.CompilerParams(vmem_limit_bytes=1024 * 1024),
    )(*held)
    return (
        state.reshape(ssm_state.shape), divergence.reshape(SEQS), logprob.reshape(SEQS), roll_z, roll_x, roll_bc,
        dt_rows.T, roll_out,
    )


def solution(mesh):
    spread = P("group", "head")
    return jax.shard_map(
        shards,
        mesh=mesh,
        in_specs=(
            P("group", None), P("group", "head", None, None), P("group", None, "head"), P("group", None, None),
            P("group"), spread, spread, spread, P("group", None), spread, spread, P("head", "group"),
            P(None, "head"), P("head"), P(), P(), P("head"), P("head"), P("head"), P(), P("head"), P(),
        ),
        out_specs=(
            P("group", "head", None, None), P("group"), P("group"), P(None, "head"), P(None, "head"), P(),
            P(None, "head"), P(None, "head"),
        ),
        check_vma=False,
    )
```

profile of v0, /device:TPU:1, one launch (start us, length us, event | category | flops | bytes accessed | tf_op | source)
XLA Modules:
  0.0 92.0 jit_solution(12644992283295980344)
XLA Ops:
  0.6 85.4 %shard_map.269 = (f32[16,640,128]{2,1,0:T(8,128)S(1)}, f32[1,16]{1,0:T(1,128)S(1)}, f32[1,16]{1,0:T(1,128)S(1)}, bf16[2560,640]{1,0:T(8,128)(2,1)S(1)}, bf16[256...) custom-call(bf16[16,2560]{1,0:T(8,128)(2,1)} %hidden_in.1, ...), custom_call_target="tpu_custom_call" | custom-call | tf_op jit(solution)/shard_map/pallas_call | solution.py:501
  86.1 5.9 %shard_map.270 = (f32[16,640,128]{2,1,0:T(8,128)}, f32[1,16]{1,0:T(1,128)}, f32[1,16]{1,0:T(1,128)}, bf16[2560,640]{1,0:T(8,128)(2,1)}, bf16[2560,640]{1,0:T(8,1...) custom-call(f32[16,640,128]{2,1,0:T(8,128)S(1)} %get-tuple-element.24.refs_0_, ...), custom_call_target="tpu_custom_call" | custom-call | tf_op jit(solution)/shard_map/pallas_call | solution.py:562
where the time goes:
time: 92.1 us; the launch traced here: 92 us
  Pallas kernels  91.3 us (99%)
    pallas_call x1, Pallas kernels, shards(): pl.pallas_call(kernel, out_shape=tuple((pltpu.VMEM(shape, dtype) for shap...  85.4 us
    pallas_call x1, Pallas kernels, shards(): pl.pallas_call(write_out, out_shape=tuple((jax.ShapeDtypeStruct(shape, dt...  5.9 us

commit v1 on v0

v1 whole, which is shorter than its diff:
```python
import functools

import jax
import jax.numpy as jnp
from jax import lax
from jax.experimental import pallas as pl
from jax.experimental.pallas import tpu as pltpu
from jax.sharding import PartitionSpec as P

MESH = pl.DeviceIdType.MESH
EPSILON = 1e-05
SEQS, D, DI, HEADS, P_SIZE, N = 16, 2560, 640, 10, 64, 128
SHARD = 160
SLICE = 320
CHIPS = 8
VL = 3200
F32 = jnp.float32
BF16 = jnp.bfloat16

PIECES = {
    "X": ("x", 0, 160),
    "OL": ("o", 0, 80),
    "DT": ("d", 0, 160),
    "Z": ("z", 0, 160),
    "BC": ("b", 0, 160),
    "OH": ("o", 80, 80),
}
ORDER = {name: at for at, name in enumerate(PIECES)}
ARRAYS = "xobdz"


def silu(v):
    return v / (1.0 + jnp.exp(-v))


def per_head(values):
    rows = values.shape[0]
    lane = lax.broadcasted_iota(jnp.int32, (rows, 128), 1)
    parts = []
    for pair in range(HEADS // 2):
        left = jnp.broadcast_to(values[:, 2 * pair : 2 * pair + 1], (rows, 128))
        right = jnp.broadcast_to(values[:, 2 * pair + 1 : 2 * pair + 2], (rows, 128))
        parts.append(jnp.where(lane < P_SIZE, left, right))
    return jnp.concatenate(parts, axis=1)


def as_column(row):
    r = lax.broadcasted_iota(jnp.int32, (SEQS, SEQS), 0)
    c = lax.broadcasted_iota(jnp.int32, (SEQS, SEQS), 1)
    return jnp.sum(jnp.where(r == c, jnp.broadcast_to(row, (SEQS, SEQS)), 0.0), axis=1, keepdims=True)


def as_row(column):
    r = lax.broadcasted_iota(jnp.int32, (SEQS, 128), 0)
    c = lax.broadcasted_iota(jnp.int32, (SEQS, 128), 1)
    return jnp.sum(jnp.where(r == c, jnp.broadcast_to(column, (SEQS, 128)), 0.0), axis=0, keepdims=True)


def two_parts(values, width):
    high = values.astype(BF16).astype(F32)
    rows = values.shape[0]
    lane = lax.broadcasted_iota(jnp.int32, (rows, 2 * width), 1)
    return jnp.where(
        lane < width, jnp.broadcast_to(high, (rows, 2 * width)), jnp.broadcast_to(values - high, (rows, 2 * width))
    ).astype(BF16)


def kernel(
    hidden_in, state_in, conv_x_in, conv_bc_in, tokens_in, ref_in, in_z, in_x, in_bc, dt_in, out_t, lm_in,
    conv_wx_in, conv_bx, conv_wbc_in, conv_bbc_in, dt_bias_in, a_log_in, skip_in, norm_in, norm_gain, final_gain,
    state, div_out, logprob_out, zg, xg, bg, dt_out, og,
    dg, lm, refs, hsend, hrecv, gains, psend, precv, gsend, grecv, rsend, rrecv, usend, urecv, lsend, lrecv,
    ssend, srecv, decays, b_rows, x_cols, c_rows, y_acc,
    hidden, conv_x, conv_bc, tokens, in_dt, conv_wx, conv_wbc, conv_bbc, dt_bias, a_log, skip_gain,
    long_rows, short_rows, small, loc, chain_s, chain_r, ag_s, ag_r, d2_s, d2_own, d2_r,
):
    g = lax.axis_index("group")
    h = lax.axis_index("head")
    k = g // 2
    c = g % 2
    x = k // 2
    zl = k % 2
    sibling = (2 * k + 1 - c, h)

    barrier = pltpu.get_barrier_semaphore()
    for d in range(1, 8):
        pl.semaphore_signal(barrier, inc=1, device_id=(g, (h + d) % 8), device_id_type=MESH)
        pl.semaphore_signal(barrier, inc=1, device_id=(2 * ((k + d) % 8) + c, h), device_id_type=MESH)
    pl.semaphore_signal(barrier, inc=1, device_id=sibling, device_id_type=MESH)

    rows_mine = pl.ds(pl.multiple_of(g * SHARD, SHARD), SHARD)
    lm_mine = pl.ds(pl.multiple_of(c * SHARD, SHARD), SHARD)
    lm_other = pl.ds(pl.multiple_of((1 - c) * SHARD, SHARD), SHARD)
    first = [
        pltpu.make_async_copy(source, target, small.at[at])
        for at, (source, target) in enumerate(
            [
                (hidden_in, hidden), (norm_in, long_rows.at[0]), (dt_in, in_dt), (final_gain, long_rows.at[1]),
                (conv_x_in, conv_x), (conv_bc_in, conv_bc), (tokens_in, tokens), (conv_wx_in, conv_wx),
                (conv_wbc_in, conv_wbc), (conv_bbc_in, conv_bbc), (dt_bias_in, dt_bias), (a_log_in, a_log),
                (skip_in, skip_gain), (conv_bx, short_rows.at[0]), (norm_gain, short_rows.at[1]),
            ]
        )
    ]
    local = [
        pltpu.make_async_copy(source, target, loc.at[at])
        for at, (source, target) in enumerate(
            [
                (in_x, xg.at[rows_mine]), (in_bc, bg.at[rows_mine]), (in_z, zg.at[rows_mine]),
                (out_t, og.at[rows_mine]), (lm_in, lm.at[lm_mine]), (state_in, state), (ref_in, refs),
            ]
        )
    ]
    for copy in first + local:
        copy.start()
    first[0].wait()

    for j in range(CHIPS):
        hsend[j] = hidden[:, SLICE * j : SLICE * (j + 1)]

    pl.semaphore_wait(barrier, 15)

    def chain_copy(phase, src, dst, device):
        return pltpu.make_async_remote_copy(
            src_ref=src, dst_ref=dst, send_sem=chain_s.at[phase], recv_sem=chain_r.at[phase],
            device_id=device, device_id_type=MESH,
        )

    pending = []

    def to_chips(phase, send_slot, recv):
        for d in range(1, 8):
            j = (k + d) % 8
            chain_copy(phase, send_slot(j), recv.at[k], (2 * j + c, h)).start()
        pending.append(chain_copy(phase, recv.at[pl.ds(0, 7)], recv.at[pl.ds(0, 7)], sibling))

    def to_heads(phase, send_slot, recv):
        for d in range(1, 8):
            j = (h + d) % 8
            chain_copy(phase, send_slot(j), recv.at[h], (g, j)).start()
        pending.append(chain_copy(phase, recv.at[pl.ds(0, 7)], recv.at[pl.ds(0, 7)], sibling))

    def received(phase, recv):
        chain_copy(phase, recv.at[pl.ds(0, 7)], recv.at[pl.ds(0, 7)], sibling).wait_recv()

    buffers = {"x": xg, "z": zg, "o": og, "b": bg, "d": dg}

    def region(piece, dx, dz, core):
        name, begin, rows = PIECES[piece]
        at = ((((x + dx) % 4) * 2 + (zl + dz) % 2) * 2 + core) * SHARD + begin
        return buffers[name].at[pl.ds(pl.multiple_of(at, 16), rows)]

    def ici(piece, dx, dz, ways):
        for way in ways:
            move = {"+": 1, "-": 3, "z": 0}[way]
            rx, rz = (dx - move) % 4, (dz + (way == "z")) % 2
            chip = ((x + move) % 4) * 2 + (zl + (way == "z")) % 2
            block = region(piece, dx, dz, c)
            pltpu.make_async_remote_copy(
                src_ref=block, dst_ref=block, send_sem=ag_s.at[ARRAYS.index(PIECES[piece][0])],
                recv_sem=ag_r.at[ORDER[piece], 4 * rz + rx - 1], device_id=(2 * chip + c, h), device_id_type=MESH,
            ).start()

    def on_chip(block, name, sem):
        pltpu.make_async_remote_copy(
            src_ref=block, dst_ref=block, send_sem=d2_s.at[ARRAYS.index(name)], recv_sem=sem,
            device_id=sibling, device_id_type=MESH,
        ).start()

    def share_own(name):
        on_chip(buffers[name].at[rows_mine], name, d2_own.at[ARRAYS.index(name)])

    def sibling_own(name):
        rows = buffers[name].at[pl.ds(pl.multiple_of((2 * k + 1 - c) * SHARD, SHARD), SHARD)]
        pltpu.make_async_remote_copy(
            src_ref=rows, dst_ref=rows, send_sem=d2_s.at[ARRAYS.index(name)], recv_sem=d2_own.at[ARRAYS.index(name)],
            device_id=sibling, device_id_type=MESH,
        ).wait_recv()

    waited = set()

    def arrived(piece, dx, dz):
        block = region(piece, dx, dz, c)
        name = PIECES[piece][0]
        pltpu.make_async_remote_copy(
            src_ref=block, dst_ref=block, send_sem=d2_s.at[ARRAYS.index(name)],
            recv_sem=ag_r.at[ORDER[piece], 4 * dz + dx - 1], device_id=sibling, device_id_type=MESH,
        ).wait_recv()
        waited.add((piece, dx, dz))
        on_chip(block, name, d2_r.at[ARRAYS.index(name)])

    to_chips(0, lambda j: hsend.at[j], hrecv)
    local[0].wait()
    share_own("x")
    local[1].wait()
    share_own("b")
    local[2].wait()
    share_own("z")
    ici("X", 0, 0, "+-")
    ici("Z", 0, 0, "z")
    hrecv[k] = hsend[k]
    for copy in first[1:]:
        copy.wait()
    turned = jnp.transpose(jnp.concatenate([in_dt[...].astype(F32), jnp.zeros((128 - HEADS, SHARD), F32)], axis=0))
    dg[rows_mine, :] = turned.astype(BF16)
    for j in range(CHIPS):
        gains[0, j] = long_rows[0:1, SLICE * j : SLICE * (j + 1)]
        gains[1, j] = long_rows[1:2, SLICE * j : SLICE * (j + 1)]
    whole = hidden[...].astype(F32)
    scale_in = lax.rsqrt(jnp.mean(whole * whole, axis=-1, keepdims=True) + EPSILON)
    share_own("d")
    local[3].wait()
    local[4].wait()

    received(0, hrecv)
    gain = gains[0, k]
    lhs = (hrecv[...].astype(F32) * gain[None]).astype(BF16).reshape(CHIPS * SEQS, SLICE)
    slice_rows = pl.ds(pl.multiple_of(k * SLICE, SLICE), SLICE)

    def partial(weights, at, width):
        product = jnp.dot(lhs, weights[slice_rows, :], preferred_element_type=F32)
        psend[:, :, at : at + width] = product.astype(BF16).reshape(CHIPS, SEQS, width)

    sibling_own("x")
    partial(xg, 0, 640)
    sibling_own("b")
    partial(bg, 640, 256)
    sibling_own("d")
    partial(dg, 896, 128)
    to_chips(1, lambda j: psend.at[j, :, pl.ds(0, 1024)], precv.at[:, :, pl.ds(0, 1024)])
    sibling_own("z")
    partial(zg, 1024, 640)
    to_chips(2, lambda j: psend.at[j, :, pl.ds(1024, 640)], precv.at[:, :, pl.ds(1024, 640)])
    precv[k] = psend[k]
    arrived("Z", 0, 1)
    ici("Z", 0, 0, "+-")
    ici("OL", 0, 0, "+-")
    ici("X", 0, 0, "z")
    ici("BC", 0, 0, "z")
    share_own("o")
    lm_copy = pltpu.make_async_remote_copy(
        src_ref=lm.at[lm_mine], dst_ref=lm.at[lm_mine], send_sem=loc.at[7], recv_sem=loc.at[8],
        device_id=sibling, device_id_type=MESH,
    )
    lm_copy.start()

    received(1, precv.at[:, :, pl.ds(0, 1024)])
    summed = jnp.sum(precv[:, :, 0:1024].astype(F32), axis=0) * scale_in
    x_new = summed[:, 0:640]
    bc_new = summed[:, 640:896]
    step_raw = summed[:, 896 : 896 + HEADS]
    acc = x_new * conv_wx[3:4, :] + short_rows[0:1, :]
    acc_bc = bc_new * conv_wbc[3:4, :] + conv_bbc[...]
    for tap in range(3):
        acc = acc + conv_x[tap].astype(F32) * conv_wx[tap : tap + 1, :]
        acc_bc = acc_bc + conv_bc[tap].astype(F32) * conv_wbc[tap : tap + 1, :]
    x_conv = silu(acc)
    bc_conv = silu(acc_bc)
    b_rows[...] = bc_conv[:, :N]
    c_vals = bc_conv[:, N:]
    biased = step_raw + dt_bias[...]
    step = jnp.maximum(biased, 0.0) + jnp.log1p(jnp.exp(-jnp.abs(biased)))
    decay = jnp.exp(-step * jnp.exp(a_log[...]))
    square = jnp.concatenate(
        [jnp.concatenate([decay, jnp.zeros((SEQS, 128 - HEADS), F32)], axis=1), jnp.zeros((112, 128), F32)], axis=0
    )
    decays[...] = jnp.transpose(square)[0:SEQS]
    inflow = per_head(step) * x_conv
    x_cols[...] = jnp.transpose(jnp.concatenate([inflow, jnp.zeros((112, DI), F32)], axis=0))
    c_high = c_vals.astype(BF16)
    c_low = (c_vals - c_high.astype(F32)).astype(BF16)
    c_rows[...] = jnp.concatenate([c_high, c_low], axis=0)
    local[5].wait()

    def two_heads(pair, _):
        rows = pl.ds(pl.multiple_of(pair * 128, 128), 128)
        columns = x_cols[rows, :]
        left = decays[pl.ds(2 * pair, 1), :]
        right = decays[pl.ds(2 * pair + 1, 1), :]
        both = c_rows[...]
        row = lax.broadcasted_iota(jnp.int32, (SEQS, N), 0)
        total = jnp.zeros((SEQS, N), F32)
        for s in range(SEQS):
            factor = jnp.concatenate(
                [
                    jnp.broadcast_to(left[:, s : s + 1], (P_SIZE, N)),
                    jnp.broadcast_to(right[:, s : s + 1], (P_SIZE, N)),
                ],
                axis=0,
            )
            column = jnp.broadcast_to(columns[:, s : s + 1], (2 * P_SIZE, N))
            new = state[s, rows, :] * factor + column * b_rows[s : s + 1, :]
            state[s, rows, :] = new
            seen = lax.dot_general(both, new.astype(BF16), (((1,), (1,)), ((), ())), preferred_element_type=F32)
            total = total + jnp.where(row == s, seen[0:SEQS] + seen[SEQS:], 0.0)
        y_acc[:, rows] = total
        return 0

    lax.fori_loop(0, HEADS // 2, two_heads, 0)
    received(2, precv.at[:, :, pl.ds(1024, 640)])
    gate = jnp.sum(precv[:, :, 1024:1664].astype(F32), axis=0) * scale_in
    ssm_out = y_acc[...] + per_head(skip_gain[...]) * x_conv
    gated = ssm_out * silu(gate)
    squares = jnp.sum(gated * gated, axis=-1, keepdims=True)
    gsend[:, 0:640] = (gated * short_rows[1:2, :]).astype(BF16)
    gsend[:, 640:768] = two_parts(squares, 64)

    to_chips(3, lambda j: gsend, grecv)
    grecv[k] = gsend[...]
    arrived("X", 3, 0)
    arrived("X", 1, 0)
    ici("X", 3, 0, "z")
    ici("X", 3, 0, "+")
    ici("Z", 0, 1, "+-")
    ici("BC", 0, 0, "+-")
    ici("DT", 0, 0, "+-")
    ici("OH", 0, 0, "z")
    ici("DT", 0, 0, "z")

    sibling_own("o")
    received(3, grecv)
    mixed = lax.dot_general(
        grecv[:, :, 0:640].reshape(CHIPS * SEQS, 640), og[slice_rows, :], (((1,), (1,)), ((), ())),
        preferred_element_type=F32,
    )
    parts = grecv[:, :, 640:768].astype(F32)
    sq = (parts[:, :, 0:1] + parts[:, :, 64:65]).reshape(CHIPS * SEQS, 1)
    rsend[:, :, 0:SLICE] = mixed.astype(BF16).reshape(CHIPS, SEQS, SLICE)
    rsend[:, :, SLICE:384] = two_parts(sq, 32).reshape(CHIPS, SEQS, 64)
    to_heads(4, lambda j: rsend.at[j], rrecv)
    rrecv[h] = rsend[h]
    ici("OH", 0, 0, "+-")
    arrived("Z", 3, 0)
    ici("Z", 3, 0, "+")
    ici("X", 1, 0, "z")
    received(4, rrecv)
    total = jnp.sum(rrecv[...].astype(F32), axis=0)
    scale_gate = lax.rsqrt((total[:, SLICE : SLICE + 1] + total[:, SLICE + 32 : SLICE + 33]) / (8.0 * DI) + EPSILON)
    stream = hrecv[h].astype(F32) + total[:, 0:SLICE] * scale_gate
    usend[:, 0:SLICE] = (stream * gains[1, k]).astype(BF16)
    usend[:, SLICE:384] = two_parts(jnp.sum(stream * stream, axis=-1, keepdims=True), 32)

    to_heads(5, lambda j: usend, urecv)
    urecv[h] = usend[...]
    arrived("Z", 1, 1)
    ici("Z", 1, 1, "-")
    arrived("OL", 1, 0)
    ici("OL", 1, 0, "-")

    local[6].wait()
    pltpu.make_async_remote_copy(
        src_ref=lm.at[lm_other], dst_ref=lm.at[lm_other], send_sem=loc.at[7], recv_sem=loc.at[8],
        device_id=sibling, device_id_type=MESH,
    ).wait_recv()
    received(5, urecv)
    final = urecv[:, :, 0:SLICE].reshape(CHIPS * SEQS, SLICE)

    def some_logits(block, _):
        at = pl.ds(pl.multiple_of(block * 640, 640), 640)
        product = jnp.dot(final, lm[:, at], preferred_element_type=F32)
        lsend[:, :, at] = product.astype(BF16).reshape(CHIPS, SEQS, 640)
        return 0

    cut = 1920
    lax.fori_loop(0, cut // 640, some_logits, 0)
    to_chips(6, lambda j: lsend.at[j, :, pl.ds(0, cut)], lrecv.at[:, :, pl.ds(0, cut)])
    lax.fori_loop(cut // 640, VL // 640, some_logits, 0)
    lsend[:, :, VL : VL + 64] = urecv[:, :, SLICE:384]
    lsend[:, :, VL + 64 : VL + 128] = urecv[:, :, SLICE:384]
    to_chips(8, lambda j: lsend.at[j, :, pl.ds(cut, VL + 128 - cut)], lrecv.at[:, :, pl.ds(cut, VL + 128 - cut)])
    lrecv[k] = lsend[k]

    ici("OL", 0, 0, "z")
    arrived("X", 2, 0)
    ici("X", 2, 0, "z")
    arrived("OL", 3, 0)
    ici("OL", 1, 0, "z")
    ici("OL", 3, 0, "z")
    arrived("BC", 0, 1)
    ici("BC", 0, 1, "+-")
    arrived("OH", 0, 1)
    ici("OH", 0, 1, "+-")
    arrived("DT", 0, 1)
    ici("DT", 0, 1, "+-")
    arrived("DT", 1, 0)
    ici("DT", 1, 0, "-")
    arrived("BC", 3, 0)
    ici("BC", 3, 0, "+")
    arrived("OH", 3, 0)
    ici("OH", 3, 0, "+")

    reference = refs[...].astype(F32)
    ref_max = jnp.max(reference, axis=-1, keepdims=True)
    weight = jnp.exp(reference - ref_max)
    ref_sum = jnp.sum(weight, axis=-1, keepdims=True)
    token = as_column(tokens[...].astype(F32)).astype(jnp.int32)

    received(6, lrecv.at[:, :, pl.ds(0, cut)])
    received(8, lrecv.at[:, :, pl.ds(cut, VL + 128 - cut)])
    logits = jnp.sum(lrecv[:, :, 0:VL].astype(F32), axis=0)
    tail = jnp.sum(lrecv[:, :, VL : VL + 128].astype(F32), axis=0)
    logits = logits * lax.rsqrt((tail[:, 0:1] + tail[:, 32:33]) / D + EPSILON)
    roll_max = jnp.max(logits, axis=-1, keepdims=True)
    roll_sum = jnp.sum(jnp.exp(logits - roll_max), axis=-1, keepdims=True)
    cross = jnp.sum(weight * (reference - logits), axis=-1, keepdims=True)
    column = lax.broadcasted_iota(jnp.int32, (SEQS, VL), 1) + h * VL
    picked = jnp.sum(jnp.where(column == token, logits, 0.0), axis=-1, keepdims=True)
    lane = lax.broadcasted_iota(jnp.int32, (SEQS, 128), 1)
    packed = jnp.zeros((SEQS, 128), F32)
    for at, value in enumerate((roll_max, roll_sum, ref_max, ref_sum, cross, picked)):
        packed = jnp.where(lane == at, jnp.broadcast_to(value, (SEQS, 128)), packed)
    ssend[...] = packed

    to_heads(7, lambda j: ssend, srecv)
    srecv[h] = ssend[...]

    arrived("BC", 1, 1)
    ici("BC", 1, 1, "-")
    arrived("OH", 1, 1)
    ici("OH", 1, 1, "-")
    arrived("DT", 1, 1)
    ici("DT", 1, 1, "-")
    arrived("OL", 2, 0)
    ici("OL", 2, 0, "z")

    received(7, srecv)
    every = srecv[...]
    m_all, s_all, rm_all, rs_all, x_all, p_all = (every[:, :, at : at + 1] for at in range(6))
    roll_top = jnp.max(m_all, axis=0)
    roll_total = jnp.sum(s_all * jnp.exp(m_all - roll_top[None]), axis=0)
    ref_top = jnp.max(rm_all, axis=0)
    ref_scale = jnp.exp(rm_all - ref_top[None])
    ref_total = jnp.sum(rs_all * ref_scale, axis=0)
    cross_total = jnp.sum(x_all * ref_scale, axis=0)
    lse_roll = roll_top + jnp.log(roll_total)
    lse_ref = ref_top + jnp.log(ref_total)
    divergence = cross_total / ref_total - lse_ref + lse_roll
    logprob = jnp.sum(p_all, axis=0) - lse_roll
    div_out[...] = as_row(divergence)[:, 0:SEQS]
    logprob_out[...] = as_row(logprob)[:, 0:SEQS]

    for piece in PIECES:
        for dz in range(2):
            for dx in range(4):
                if (dx, dz) != (0, 0) and (piece, dx, dz) not in waited:
                    arrived(piece, dx, dz)
    seven, eight = pl.ds(0, 7 * SHARD), pl.ds(0, 8 * SHARD)
    for at, name in enumerate(ARRAYS):
        whole = buffers[name].at[seven]
        pltpu.make_async_remote_copy(
            src_ref=whole, dst_ref=whole, send_sem=ag_s.at[at], recv_sem=d2_r.at[at], device_id=sibling,
            device_id_type=MESH,
        ).wait()
    for block in range(2):
        turned = jnp.transpose(dg[block * 1280 : (block + 1) * 1280, :].astype(F32))
        dt_out[:, block * 1280 : (block + 1) * 1280] = turned[0:HEADS].astype(BF16)
    for at, name in enumerate(ARRAYS):
        whole = buffers[name].at[eight]
        pltpu.make_async_remote_copy(
            src_ref=whole, dst_ref=whole, send_sem=d2_s.at[at], recv_sem=d2_r.at[at], device_id=sibling,
            device_id_type=MESH,
        ).wait_send()
    lm_copy.wait_send()
    for copy in pending:
        copy.wait_send()


def write_out(*refs):
    count = len(refs) // 2
    copies = [pltpu.make_async_copy(refs[at], refs[count + at], refs[-1].at[at]) for at in range(count)]
    for copy in copies:
        copy.start()
    for copy in copies:
        copy.wait()


ANY = pl.BlockSpec(memory_space=pl.ANY)
VMEM = pl.BlockSpec(memory_space=pltpu.VMEM)


def shards(
    hidden_in, ssm_state, conv_x_state, conv_bc_state, token_ids, ref_logits, in_z, in_x, in_bc, in_dt, out_t,
    lm_head, conv_wx, conv_bx, conv_wbc, conv_bbc, dt_bias, a_log, skip_gain, norm_in, norm_gain, final_gain,
):
    row = lambda v: v.reshape(1, -1)
    results = (
        ((SEQS, DI, N), F32), ((1, SEQS), F32), ((1, SEQS), F32), ((D, DI), BF16), ((D, DI), BF16), ((D, 256), BF16),
        ((HEADS, D), BF16), ((D, DI), BF16),
    )
    held = pl.pallas_call(
        kernel,
        out_shape=tuple(pltpu.VMEM(shape, dtype) for shape, dtype in results),
        in_specs=[pl.BlockSpec(memory_space=pltpu.HBM)] * 22,
        out_specs=(VMEM,) * len(results),
        scratch_shapes=[
            pltpu.VMEM((D, 128), BF16),
            pltpu.VMEM((SLICE, VL), BF16),
            pltpu.VMEM((SEQS, VL), BF16),
            pltpu.VMEM((CHIPS, SEQS, SLICE), BF16),
            pltpu.VMEM((CHIPS, SEQS, SLICE), BF16),
            pltpu.VMEM((2, CHIPS, 1, SLICE), F32),
            pltpu.VMEM((CHIPS, SEQS, 1664), BF16),
            pltpu.VMEM((CHIPS, SEQS, 1664), BF16),
            pltpu.VMEM((SEQS, 768), BF16),
            pltpu.VMEM((CHIPS, SEQS, 768), BF16),
            pltpu.VMEM((CHIPS, SEQS, 384), BF16),
            pltpu.VMEM((CHIPS, SEQS, 384), BF16),
            pltpu.VMEM((SEQS, 384), BF16),
            pltpu.VMEM((CHIPS, SEQS, 384), BF16),
            pltpu.VMEM((CHIPS, SEQS, VL + 128), BF16),
            pltpu.VMEM((CHIPS, SEQS, VL + 128), BF16),
            pltpu.VMEM((SEQS, 128), F32),
            pltpu.VMEM((CHIPS, SEQS, 128), F32),
            pltpu.VMEM((SEQS, 128), F32),
            pltpu.VMEM((SEQS, N), F32),
            pltpu.VMEM((DI, 128), F32),
            pltpu.VMEM((2 * SEQS, N), BF16),
            pltpu.VMEM((SEQS, DI), F32),
            pltpu.VMEM((SEQS, D), BF16),
            pltpu.VMEM((3, SEQS, DI), BF16),
            pltpu.VMEM((3, SEQS, 256), BF16),
            pltpu.VMEM((1, SEQS), jnp.int32),
            pltpu.VMEM((HEADS, SHARD), BF16),
            pltpu.VMEM((4, DI), F32),
            pltpu.VMEM((4, 256), F32),
            pltpu.VMEM((1, 256), F32),
            pltpu.VMEM((1, HEADS), F32),
            pltpu.VMEM((1, HEADS), F32),
            pltpu.VMEM((1, HEADS), F32),
            pltpu.VMEM((2, D), F32),
            pltpu.VMEM((2, DI), F32),
            pltpu.SemaphoreType.DMA((15,)),
            pltpu.SemaphoreType.DMA((9,)),
            pltpu.SemaphoreType.DMA((9,)),
            pltpu.SemaphoreType.DMA((9,)),
            pltpu.SemaphoreType.DMA((5,)),
            pltpu.SemaphoreType.DMA((6, 7)),
            pltpu.SemaphoreType.DMA((5,)),
            pltpu.SemaphoreType.DMA((5,)),
            pltpu.SemaphoreType.DMA((5,)),
        ],
        compiler_params=pltpu.CompilerParams(
            collective_id=0, has_side_effects=True, vmem_limit_bytes=32 * 1024 * 1024
        ),
    )(*[pltpu.with_memory_space_constraint(array, pltpu.HBM) for array in (
        hidden_in, ssm_state.reshape(SEQS, DI, N), conv_x_state.transpose(1, 0, 2), conv_bc_state.transpose(1, 0, 2),
        row(token_ids), ref_logits, in_z, in_x, in_bc, in_dt.T, out_t, lm_head.T,
        conv_wx, conv_bx, conv_wbc, row(conv_bbc), row(dt_bias), row(a_log), row(skip_gain), norm_in,
        norm_gain, final_gain,
    )])
    held = [pltpu.with_memory_space_constraint(array, pltpu.VMEM) for array in held]
    state, divergence, logprob, roll_z, roll_x, roll_bc, dt_rows, roll_out = pl.pallas_call(
        write_out,
        out_shape=tuple(jax.ShapeDtypeStruct(shape, dtype) for shape, dtype in results),
        in_specs=[VMEM] * len(results),
        out_specs=(ANY,) * len(results),
        scratch_shapes=[pltpu.SemaphoreType.DMA((len(results),))],
        compiler_params=pltpu.CompilerParams(vmem_limit_bytes=1024 * 1024),
    )(*held)
    return (
        state.reshape(ssm_state.shape), divergence.reshape(SEQS), logprob.reshape(SEQS), roll_z, roll_x, roll_bc,
        dt_rows.T, roll_out,
    )


def solution(mesh):
    spread = P("group", "head")
    return jax.shard_map(
        shards,
        mesh=mesh,
        in_specs=(
            P("group", None), P("group", "head", None, None), P("group", None, "head"), P("group", None, None),
            P("group"), spread, spread, spread, P("group", None), spread, spread, P("head", "group"),
            P(None, "head"), P("head"), P(), P(), P("head"), P("head"), P("head"), P(), P("head"), P(),
        ),
        out_specs=(
            P("group", "head", None, None), P("group"), P("group"), P(None, "head"), P(None, "head"), P(),
            P(None, "head"), P(None, "head"),
        ),
        check_vma=False,
    )
```

time: 92.1 us -> 80.3 us (0.87)
  Pallas kernels: 91.3 us -> 79.5 us
    pallas_call x1, Pallas kernels: 85.4 us -> 73.6 us  [shards(): pl.pallas_call(kernel, out_shape=tuple((pltpu.VMEM(shape, dtype) for shap...]
where the time goes in v1:
time: 80.3 us; the launch traced here: 80.1 us
  Pallas kernels  79.5 us (99%)
    pallas_call x1, Pallas kernels, shards(): pl.pallas_call(kernel, out_shape=tuple((pltpu.VMEM(shape, dtype) for shap...  73.6 us
    pallas_call x1, Pallas kernels, shards(): pl.pallas_call(write_out, out_shape=tuple((jax.ShapeDtypeStruct(shape, dt...  5.9 us

profile of v1, /device:TPU:1, one launch (start us, length us, event | category | flops | bytes accessed | tf_op | source)
XLA Modules:
  0.0 80.1 jit_solution(17481086805797765050)
XLA Ops:
  0.6 73.6 %shard_map.269 = (f32[16,640,128]{2,1,0:T(8,128)S(1)}, f32[1,16]{1,0:T(1,128)S(1)}, f32[1,16]{1,0:T(1,128)S(1)}, bf16[2560,640]{1,0:T(8,128)(2,1)S(1)}, bf16[256...) custom-call(bf16[16,2560]{1,0:T(8,128)(2,1)} %hidden_in.1, ...), custom_call_target="tpu_custom_call" | custom-call | tf_op jit(solution)/shard_map/pallas_call | solution.py:490
  74.2 5.9 %shard_map.270 = (f32[16,640,128]{2,1,0:T(8,128)}, f32[1,16]{1,0:T(1,128)}, f32[1,16]{1,0:T(1,128)}, bf16[2560,640]{1,0:T(8,128)(2,1)}, bf16[2560,640]{1,0:T(8,1...) custom-call(f32[16,640,128]{2,1,0:T(8,128)S(1)} %get-tuple-element.24.refs_0_, ...), custom_call_target="tpu_custom_call" | custom-call | tf_op jit(solution)/shard_map/pallas_call | solution.py:552

commit v2 on v1

--- a/solution.py
+++ b/solution.py
@@ -19,11 +19,11 @@
 
 PIECES = {
     "X": ("x", 0, 160),
-    "OL": ("o", 0, 80),
+    "OL": ("o", 0, 64),
     "DT": ("d", 0, 160),
     "Z": ("z", 0, 160),
     "BC": ("b", 0, 160),
-    "OH": ("o", 80, 80),
+    "OH": ("o", 64, 96),
 }
 ORDER = {name: at for at, name in enumerate(PIECES)}
 ARRAYS = "xobdz"
@@ -69,10 +69,10 @@
     hidden_in, state_in, conv_x_in, conv_bc_in, tokens_in, ref_in, in_z, in_x, in_bc, dt_in, out_t, lm_in,
     conv_wx_in, conv_bx, conv_wbc_in, conv_bbc_in, dt_bias_in, a_log_in, skip_in, norm_in, norm_gain, final_gain,
     state, div_out, logprob_out, zg, xg, bg, dt_out, og,
-    dg, lm, refs, hsend, hrecv, gains, psend, precv, gsend, grecv, rsend, rrecv, usend, urecv, lsend, lrecv,
+    dts, lm, refs, hsend, hrecv, gains, psend, precv, gsend, grecv, rsend, rrecv, usend, urecv, lsend, lrecv,
     ssend, srecv, decays, b_rows, x_cols, c_rows, y_acc,
-    hidden, conv_x, conv_bc, tokens, in_dt, conv_wx, conv_wbc, conv_bbc, dt_bias, a_log, skip_gain,
-    long_rows, short_rows, small, loc, chain_s, chain_r, ag_s, ag_r, d2_s, d2_own, d2_r,
+    hidden, conv_x, conv_bc, tokens, conv_wx, conv_wbc, conv_bbc, dt_bias, a_log, skip_gain,
+    long_rows, short_rows, small, loc, chain_s, chain_r, ag_s, ag_r, d2_s, d2_own, d2_r, y_sems,
 ):
     g = lax.axis_index("group")
     h = lax.axis_index("head")
@@ -80,6 +80,7 @@
     c = g % 2
     x = k // 2
     zl = k % 2
+    y = h // 2
     sibling = (2 * k + 1 - c, h)
 
     barrier = pltpu.get_barrier_semaphore()
@@ -95,7 +96,7 @@
         pltpu.make_async_copy(source, target, small.at[at])
         for at, (source, target) in enumerate(
             [
-                (hidden_in, hidden), (norm_in, long_rows.at[0]), (dt_in, in_dt), (final_gain, long_rows.at[1]),
+                (hidden_in, hidden), (dt_in, dts.at[g]), (norm_in, long_rows.at[0]), (final_gain, long_rows.at[1]),
                 (conv_x_in, conv_x), (conv_bc_in, conv_bc), (tokens_in, tokens), (conv_wx_in, conv_wx),
                 (conv_wbc_in, conv_wbc), (conv_bbc_in, conv_bbc), (dt_bias_in, dt_bias), (a_log_in, a_log),
                 (skip_in, skip_gain), (conv_bx, short_rows.at[0]), (norm_gain, short_rows.at[1]),
@@ -143,11 +144,20 @@
     def received(phase, recv):
         chain_copy(phase, recv.at[pl.ds(0, 7)], recv.at[pl.ds(0, 7)], sibling).wait_recv()
 
-    buffers = {"x": xg, "z": zg, "o": og, "b": bg, "d": dg}
+    buffers = {"x": xg, "z": zg, "o": og, "b": bg, "d": dts}
+
+    def quarter(device):
+        at = pl.multiple_of(device * SHARD + 80 * (y // 2), 16)
+        return bg.at[pl.ds(at, 80), pl.ds(pl.multiple_of(128 * (y % 2), 128), 128)]
 
     def region(piece, dx, dz, core):
         name, begin, rows = PIECES[piece]
-        at = ((((x + dx) % 4) * 2 + (zl + dz) % 2) * 2 + core) * SHARD + begin
+        at = (((x + dx) % 4) * 2 + (zl + dz) % 2) * 2 + core
+        if name == "d":
+            return dts.at[at]
+        if name == "b":
+            return quarter(at)
+        at = at * SHARD + begin
         return buffers[name].at[pl.ds(pl.multiple_of(at, 16), rows)]
 
     def ici(piece, dx, dz, ways):
@@ -167,11 +177,25 @@
             device_id=sibling, device_id_type=MESH,
         ).start()
 
+    def shard_of(name, device):
+        if name == "d":
+            return dts.at[device]
+        return buffers[name].at[pl.ds(pl.multiple_of(device * SHARD, SHARD), SHARD)]
+
+    def along_y():
+        return pltpu.make_async_remote_copy(
+            src_ref=bg.at[pl.ds(0, 840)], dst_ref=bg.at[pl.ds(0, 840)], send_sem=y_sems.at[0], recv_sem=y_sems.at[1],
+            device_id=sibling, device_id_type=MESH,
+        )
+
+    def several(name, shards):
+        return buffers[name].at[pl.ds(0, shards if name == "d" else shards * SHARD)]
+
     def share_own(name):
-        on_chip(buffers[name].at[rows_mine], name, d2_own.at[ARRAYS.index(name)])
+        on_chip(shard_of(name, g), name, d2_own.at[ARRAYS.index(name)])
 
     def sibling_own(name):
-        rows = buffers[name].at[pl.ds(pl.multiple_of((2 * k + 1 - c) * SHARD, SHARD), SHARD)]
+        rows = shard_of(name, 2 * k + 1 - c)
         pltpu.make_async_remote_copy(
             src_ref=rows, dst_ref=rows, send_sem=d2_s.at[ARRAYS.index(name)], recv_sem=d2_own.at[ARRAYS.index(name)],
             device_id=sibling, device_id_type=MESH,
@@ -187,6 +211,13 @@
             recv_sem=ag_r.at[ORDER[piece], 4 * dz + dx - 1], device_id=sibling, device_id_type=MESH,
         ).wait_recv()
         waited.add((piece, dx, dz))
+        if name == "b":
+            for move in range(1, 4):
+                pltpu.make_async_remote_copy(
+                    src_ref=block, dst_ref=block, send_sem=y_sems.at[0], recv_sem=y_sems.at[1],
+                    device_id=(g, (h + 2 * move) % 8), device_id_type=MESH,
+                ).start()
+            return
         on_chip(block, name, d2_r.at[ARRAYS.index(name)])
 
     to_chips(0, lambda j: hsend.at[j], hrecv)
@@ -196,19 +227,18 @@
     share_own("b")
     local[2].wait()
     share_own("z")
+    first[1].wait()
+    share_own("d")
     ici("X", 0, 0, "+-")
     ici("Z", 0, 0, "z")
     hrecv[k] = hsend[k]
-    for copy in first[1:]:
+    for copy in first[2:]:
         copy.wait()
-    turned = jnp.transpose(jnp.concatenate([in_dt[...].astype(F32), jnp.zeros((128 - HEADS, SHARD), F32)], axis=0))
-    dg[rows_mine, :] = turned.astype(BF16)
     for j in range(CHIPS):
         gains[0, j] = long_rows[0:1, SLICE * j : SLICE * (j + 1)]
         gains[1, j] = long_rows[1:2, SLICE * j : SLICE * (j + 1)]
     whole = hidden[...].astype(F32)
     scale_in = lax.rsqrt(jnp.mean(whole * whole, axis=-1, keepdims=True) + EPSILON)
-    share_own("d")
     local[3].wait()
     local[4].wait()
 
@@ -217,19 +247,23 @@
     lhs = (hrecv[...].astype(F32) * gain[None]).astype(BF16).reshape(CHIPS * SEQS, SLICE)
     slice_rows = pl.ds(pl.multiple_of(k * SLICE, SLICE), SLICE)
 
+    def turned(device):
+        rows = jnp.concatenate([dts[device].astype(F32), jnp.zeros((128 - HEADS, SHARD), F32)], axis=0)
+        return jnp.transpose(rows).astype(BF16)
+
     def partial(weights, at, width):
-        product = jnp.dot(lhs, weights[slice_rows, :], preferred_element_type=F32)
+        product = jnp.dot(lhs, weights, preferred_element_type=F32)
         psend[:, :, at : at + width] = product.astype(BF16).reshape(CHIPS, SEQS, width)
 
     sibling_own("x")
-    partial(xg, 0, 640)
+    partial(xg[slice_rows, :], 0, 640)
     sibling_own("b")
-    partial(bg, 640, 256)
+    partial(bg[slice_rows, :], 640, 256)
     sibling_own("d")
-    partial(dg, 896, 128)
+    partial(jnp.concatenate([turned(2 * k), turned(2 * k + 1)], axis=0), 896, 128)
     to_chips(1, lambda j: psend.at[j, :, pl.ds(0, 1024)], precv.at[:, :, pl.ds(0, 1024)])
     sibling_own("z")
-    partial(zg, 1024, 640)
+    partial(zg[slice_rows, :], 1024, 640)
     to_chips(2, lambda j: psend.at[j, :, pl.ds(1024, 640)], precv.at[:, :, pl.ds(1024, 640)])
     precv[k] = psend[k]
     arrived("Z", 0, 1)
@@ -237,6 +271,7 @@
     ici("OL", 0, 0, "+-")
     ici("X", 0, 0, "z")
     ici("BC", 0, 0, "z")
+    ici("DT", 0, 0, "z")
     share_own("o")
     lm_copy = pltpu.make_async_remote_copy(
         src_ref=lm.at[lm_mine], dst_ref=lm.at[lm_mine], send_sem=loc.at[7], recv_sem=loc.at[8],
@@ -308,14 +343,12 @@
     to_chips(3, lambda j: gsend, grecv)
     grecv[k] = gsend[...]
     arrived("X", 3, 0)
+    ici("X", 3, 0, "z+")
+    ici("DT", 0, 0, "+-")
+    ici("BC", 0, 0, "+-")
+    ici("Z", 0, 1, "+-")
+    ici("OH", 0, 0, "z")
     arrived("X", 1, 0)
-    ici("X", 3, 0, "z")
-    ici("X", 3, 0, "+")
-    ici("Z", 0, 1, "+-")
-    ici("BC", 0, 0, "+-")
-    ici("DT", 0, 0, "+-")
-    ici("OH", 0, 0, "z")
-    ici("DT", 0, 0, "z")
 
     sibling_own("o")
     received(3, grecv)
@@ -329,10 +362,17 @@
     rsend[:, :, SLICE:384] = two_parts(sq, 32).reshape(CHIPS, SEQS, 64)
     to_heads(4, lambda j: rsend.at[j], rrecv)
     rrecv[h] = rsend[h]
+    arrived("DT", 0, 1)
+    ici("DT", 0, 1, "+-")
+    arrived("BC", 0, 1)
+    ici("BC", 0, 1, "+-")
     ici("OH", 0, 0, "+-")
+    ici("X", 1, 0, "z")
     arrived("Z", 3, 0)
     ici("Z", 3, 0, "+")
-    ici("X", 1, 0, "z")
+    arrived("Z", 1, 0)
+    arrived("Z", 1, 1)
+    ici("Z", 1, 1, "-")
     received(4, rrecv)
     total = jnp.sum(rrecv[...].astype(F32), axis=0)
     scale_gate = lax.rsqrt((total[:, SLICE : SLICE + 1] + total[:, SLICE + 32 : SLICE + 33]) / (8.0 * DI) + EPSILON)
@@ -342,10 +382,24 @@
 
     to_heads(5, lambda j: usend, urecv)
     urecv[h] = usend[...]
-    arrived("Z", 1, 1)
-    ici("Z", 1, 1, "-")
+    arrived("DT", 1, 0)
+    ici("DT", 1, 0, "-")
+    arrived("DT", 1, 1)
+    ici("DT", 1, 1, "-")
+    arrived("BC", 3, 0)
+    ici("BC", 3, 0, "+")
+    arrived("BC", 1, 1)
+    ici("BC", 1, 1, "-")
     arrived("OL", 1, 0)
     ici("OL", 1, 0, "-")
+    ici("OL", 0, 0, "z")
+    arrived("OL", 3, 0)
+    arrived("X", 0, 1)
+    arrived("X", 3, 1)
+    arrived("BC", 1, 0)
+    arrived("BC", 3, 1)
+    arrived("DT", 3, 0)
+    arrived("DT", 3, 1)
 
     local[6].wait()
     pltpu.make_async_remote_copy(
@@ -370,24 +424,25 @@
     to_chips(8, lambda j: lsend.at[j, :, pl.ds(cut, VL + 128 - cut)], lrecv.at[:, :, pl.ds(cut, VL + 128 - cut)])
     lrecv[k] = lsend[k]
 
-    ici("OL", 0, 0, "z")
+    arrived("OH", 0, 1)
+    ici("OH", 0, 1, "+-")
     arrived("X", 2, 0)
     ici("X", 2, 0, "z")
-    arrived("OL", 3, 0)
     ici("OL", 1, 0, "z")
     ici("OL", 3, 0, "z")
-    arrived("BC", 0, 1)
-    ici("BC", 0, 1, "+-")
-    arrived("OH", 0, 1)
-    ici("OH", 0, 1, "+-")
-    arrived("DT", 0, 1)
-    ici("DT", 0, 1, "+-")
-    arrived("DT", 1, 0)
-    ici("DT", 1, 0, "-")
-    arrived("BC", 3, 0)
-    ici("BC", 3, 0, "+")
     arrived("OH", 3, 0)
     ici("OH", 3, 0, "+")
+    arrived("OL", 2, 0)
+    ici("OL", 2, 0, "z")
+    arrived("BC", 2, 0)
+    arrived("BC", 2, 1)
+    arrived("X", 1, 1)
+    arrived("Z", 3, 1)
+    arrived("OH", 1, 0)
+    arrived("DT", 2, 0)
+    arrived("DT", 2, 1)
+    arrived("Z", 2, 0)
+    arrived("Z", 2, 1)
 
     reference = refs[...].astype(F32)
     ref_max = jnp.max(reference, axis=-1, keepdims=True)
@@ -414,14 +469,17 @@
     to_heads(7, lambda j: ssend, srecv)
     srecv[h] = ssend[...]
 
-    arrived("BC", 1, 1)
-    ici("BC", 1, 1, "-")
+    along_y().wait_recv()
+    for dz in range(2):
+        for dx in range(4):
+            if (dx, dz) != (0, 0):
+                block = shard_of("b", ((((x + dx) % 4) * 2 + (zl + dz) % 2) * 2 + c))
+                on_chip(block, "b", d2_r.at[ARRAYS.index("b")])
     arrived("OH", 1, 1)
     ici("OH", 1, 1, "-")
-    arrived("DT", 1, 1)
-    ici("DT", 1, 1, "-")
-    arrived("OL", 2, 0)
-    ici("OL", 2, 0, "z")
+    arrived("OL", 0, 1)
+    arrived("X", 2, 1)
+    arrived("OH", 3, 1)
 
     received(7, srecv)
     every = srecv[...]
@@ -444,23 +502,19 @@
             for dx in range(4):
                 if (dx, dz) != (0, 0) and (piece, dx, dz) not in waited:
                     arrived(piece, dx, dz)
-    seven, eight = pl.ds(0, 7 * SHARD), pl.ds(0, 8 * SHARD)
     for at, name in enumerate(ARRAYS):
-        whole = buffers[name].at[seven]
         pltpu.make_async_remote_copy(
-            src_ref=whole, dst_ref=whole, send_sem=ag_s.at[at], recv_sem=d2_r.at[at], device_id=sibling,
-            device_id_type=MESH,
+            src_ref=bg.at[pl.ds(0, 280)] if name == "b" else several(name, 7), dst_ref=several(name, 7),
+            send_sem=ag_s.at[at], recv_sem=d2_r.at[at], device_id=sibling, device_id_type=MESH,
         ).wait()
-    for block in range(2):
-        turned = jnp.transpose(dg[block * 1280 : (block + 1) * 1280, :].astype(F32))
-        dt_out[:, block * 1280 : (block + 1) * 1280] = turned[0:HEADS].astype(BF16)
+    dt_out[...] = jnp.concatenate([dts[device].astype(F32) for device in range(2 * CHIPS)], axis=1).astype(BF16)
     for at, name in enumerate(ARRAYS):
-        whole = buffers[name].at[eight]
         pltpu.make_async_remote_copy(
-            src_ref=whole, dst_ref=whole, send_sem=d2_s.at[at], recv_sem=d2_r.at[at], device_id=sibling,
-            device_id_type=MESH,
+            src_ref=several(name, 8), dst_ref=several(name, 8), send_sem=d2_s.at[at], recv_sem=d2_r.at[at],
+            device_id=sibling, device_id_type=MESH,
         ).wait_send()
     lm_copy.wait_send()
+    along_y().wait_send()
     for copy in pending:
         copy.wait_send()
 
@@ -493,7 +547,7 @@
         in_specs=[pl.BlockSpec(memory_space=pltpu.HBM)] * 22,
         out_specs=(VMEM,) * len(results),
         scratch_shapes=[
-            pltpu.VMEM((D, 128), BF16),
+            pltpu.VMEM((2 * CHIPS, HEADS, SHARD), BF16),
             pltpu.VMEM((SLICE, VL), BF16),
             pltpu.VMEM((SEQS, VL), BF16),
             pltpu.VMEM((CHIPS, SEQS, SLICE), BF16),
@@ -520,7 +574,6 @@
             pltpu.VMEM((3, SEQS, DI), BF16),
             pltpu.VMEM((3, SEQS, 256), BF16),
             pltpu.VMEM((1, SEQS), jnp.int32),
-            pltpu.VMEM((HEADS, SHARD), BF16),
             pltpu.VMEM((4, DI), F32),
             pltpu.VMEM((4, 256), F32),
             pltpu.VMEM((1, 256), F32),
@@ -538,6 +591,7 @@
             pltpu.SemaphoreType.DMA((5,)),
             pltpu.SemaphoreType.DMA((5,)),
             pltpu.SemaphoreType.DMA((5,)),
+            pltpu.SemaphoreType.DMA((2,)),
         ],
         compiler_params=pltpu.CompilerParams(
             collective_id=0, has_side_effects=True, vmem_limit_bytes=32 * 1024 * 1024

time: 80.3 us -> 72.3 us (0.900)
  Pallas kernels: 79.5 us -> 71.5 us
    pallas_call x1, Pallas kernels: 73.6 us -> 65.6 us  [shards(): pl.pallas_call(kernel, out_shape=tuple((pltpu.VMEM(shape, dtype) for shap...]
where the time goes in v2:
time: 72.3 us; the launch traced here: 72.1 us
  Pallas kernels  71.5 us (99%)
    pallas_call x1, Pallas kernels, shards(): pl.pallas_call(kernel, out_shape=tuple((pltpu.VMEM(shape, dtype) for shap...  65.6 us
    pallas_call x1, Pallas kernels, shards(): pl.pallas_call(write_out, out_shape=tuple((jax.ShapeDtypeStruct(shape, dt...  5.9 us

profile of v2, /device:TPU:1, one launch (start us, length us, event | category | flops | bytes accessed | tf_op | source)
XLA Modules:
  0.0 72.1 jit_solution(14866125881145846245)
XLA Ops:
  0.6 65.6 %shard_map.269 = (f32[16,640,128]{2,1,0:T(8,128)S(1)}, f32[1,16]{1,0:T(1,128)S(1)}, f32[1,16]{1,0:T(1,128)S(1)}, bf16[2560,640]{1,0:T(8,128)(2,1)S(1)}, bf16[256...) custom-call(bf16[16,2560]{1,0:T(8,128)(2,1)} %hidden_in.1, ...), custom_call_target="tpu_custom_call" | custom-call | tf_op jit(solution)/shard_map/pallas_call | solution.py:544
  66.2 5.9 %shard_map.270 = (f32[16,640,128]{2,1,0:T(8,128)}, f32[1,16]{1,0:T(1,128)}, f32[1,16]{1,0:T(1,128)}, bf16[2560,640]{1,0:T(8,128)(2,1)}, bf16[2560,640]{1,0:T(8,1...) custom-call(f32[16,640,128]{2,1,0:T(8,128)S(1)} %get-tuple-element.24.refs_0_, ...), custom_call_target="tpu_custom_call" | custom-call | tf_op jit(solution)/shard_map/pallas_call | solution.py:606

commit v3 on v2

--- a/solution.py
+++ b/solution.py
@@ -14,16 +14,18 @@
 SLICE = 320
 CHIPS = 8
 VL = 3200
+CUT = 1920
+REST = VL + 128 - CUT
 F32 = jnp.float32
 BF16 = jnp.bfloat16
 
 PIECES = {
     "X": ("x", 0, 160),
-    "OL": ("o", 0, 64),
+    "OL": ("o", 0, 32),
     "DT": ("d", 0, 160),
     "Z": ("z", 0, 160),
     "BC": ("b", 0, 160),
-    "OH": ("o", 64, 96),
+    "OH": ("o", 32, 128),
 }
 ORDER = {name: at for at, name in enumerate(PIECES)}
 ARRAYS = "xobdz"
@@ -69,10 +71,10 @@
     hidden_in, state_in, conv_x_in, conv_bc_in, tokens_in, ref_in, in_z, in_x, in_bc, dt_in, out_t, lm_in,
     conv_wx_in, conv_bx, conv_wbc_in, conv_bbc_in, dt_bias_in, a_log_in, skip_in, norm_in, norm_gain, final_gain,
     state, div_out, logprob_out, zg, xg, bg, dt_out, og,
-    dts, lm, refs, hsend, hrecv, gains, psend, precv, gsend, grecv, rsend, rrecv, usend, urecv, lsend, lrecv,
+    dts, lm, refs, hsend, hrecv, gains, psend, precv, gsend, grecv, rsend, rrecv, usend, urecv, lsend, zrecv, zsum, total_z, xrecv, xsum, total_x,
     ssend, srecv, decays, b_rows, x_cols, c_rows, y_acc,
     hidden, conv_x, conv_bc, tokens, conv_wx, conv_wbc, conv_bbc, dt_bias, a_log, skip_gain,
-    long_rows, short_rows, small, loc, chain_s, chain_r, ag_s, ag_r, d2_s, d2_own, d2_r, y_sems,
+    long_rows, short_rows, small, loc, chain_s, chain_r, ag_s, ag_r, d2_s, d2_own, d2_r, y_sems, sum_s, sum_r,
 ):
     g = lax.axis_index("group")
     h = lax.axis_index("head")
@@ -409,20 +411,67 @@
     received(5, urecv)
     final = urecv[:, :, 0:SLICE].reshape(CHIPS * SEQS, SLICE)
 
-    def some_logits(block, _):
-        at = pl.ds(pl.multiple_of(block * 640, 640), 640)
-        product = jnp.dot(final, lm[:, at], preferred_element_type=F32)
-        lsend[:, :, at] = product.astype(BF16).reshape(CHIPS, SEQS, 640)
-        return 0
-
-    cut = 1920
-    lax.fori_loop(0, cut // 640, some_logits, 0)
-    to_chips(6, lambda j: lsend.at[j, :, pl.ds(0, cut)], lrecv.at[:, :, pl.ds(0, cut)])
-    lax.fori_loop(cut // 640, VL // 640, some_logits, 0)
-    lsend[:, :, VL : VL + 64] = urecv[:, :, SLICE:384]
-    lsend[:, :, VL + 64 : VL + 128] = urecv[:, :, SLICE:384]
-    to_chips(8, lambda j: lsend.at[j, :, pl.ds(cut, VL + 128 - cut)], lrecv.at[:, :, pl.ds(cut, VL + 128 - cut)])
-    lrecv[k] = lsend[k]
+    def some_logits(at, width):
+        product = jnp.dot(final, lm[:, at : at + width], preferred_element_type=F32)
+        product = product.astype(BF16).reshape(4, 2, SEQS, width)
+        for z in range(2):
+            lsend[z, :, :, at : at + width] = product[:, z]
+
+    def sum_copy(at, src, dst, device):
+        return pltpu.make_async_remote_copy(
+            src_ref=src, dst_ref=dst, send_sem=sum_s.at[at], recv_sem=sum_r.at[at], device_id=device,
+            device_id_type=MESH,
+        )
+
+    partner = (2 * (2 * x + 1 - zl) + c, h)
+    across = []
+    for part in range(3):
+        columns = pl.ds(640 * part, 640)
+        some_logits(640 * part, 640)
+        copy = sum_copy(part, lsend.at[1 - zl, :, :, columns], zrecv.at[:, :, columns], partner)
+        copy.start()
+        across.append(copy)
+        if part == 0:
+            for at in range(CUT, VL, 640):
+                some_logits(at, 640)
+            for z in range(2):
+                for position in range(4):
+                    lsend[z, position, :, VL : VL + 64] = urecv[2 * position + z, :, SLICE:384]
+                    lsend[z, position, :, VL + 64 : VL + 128] = urecv[2 * position + z, :, SLICE:384]
+            for move in (1, 3, 2):
+                other = (x + move) % 4
+                sum_copy(3, lsend.at[:, other, :, pl.ds(CUT, REST)], xrecv.at[x], (2 * (2 * other + zl) + c, h)).start()
+
+    reference = refs[...].astype(F32)
+    ref_max = jnp.max(reference, axis=-1, keepdims=True)
+    weight = jnp.exp(reference - ref_max)
+    ref_sum = jnp.sum(weight, axis=-1, keepdims=True)
+    token = as_column(tokens[...].astype(F32)).astype(jnp.int32)
+
+
+    def pair_sums(part):
+        columns = slice(640 * part, 640 * part + 640)
+        across[part].wait_recv()
+        summed = lsend[zl, :, :, columns].astype(F32) + zrecv[:, :, columns].astype(F32)
+        zsum[:, :, columns] = summed.astype(BF16)
+        for move in (2, 1, 3):
+            other = (x + move) % 4
+            sum_copy(
+                4 + part, zsum.at[other, :, pl.ds(640 * part, 640)], total_z.at[x, :, pl.ds(640 * part, 640)],
+                (2 * (2 * other + zl) + c, h),
+            ).start()
+        total_z[x, :, columns] = zsum[x, :, columns]
+
+    pair_sums(0)
+    pair_sums(1)
+    three = xrecv.at[pl.ds(0, 3)]
+    xrecv[x] = lsend[:, x, :, CUT : CUT + REST]
+    sum_copy(3, three, three, partner).wait_recv()
+    xsum[...] = jnp.sum(xrecv[:, 1 - zl].astype(F32), axis=0).astype(BF16)
+    along_z = sum_copy(7, xsum, total_x, partner)
+    along_z.start()
+    mine = jnp.sum(xrecv[:, zl].astype(F32), axis=0)
+    pair_sums(2)
 
     arrived("OH", 0, 1)
     ici("OH", 0, 1, "+-")
@@ -444,16 +493,14 @@
     arrived("Z", 2, 0)
     arrived("Z", 2, 1)
 
-    reference = refs[...].astype(F32)
-    ref_max = jnp.max(reference, axis=-1, keepdims=True)
-    weight = jnp.exp(reference - ref_max)
-    ref_sum = jnp.sum(weight, axis=-1, keepdims=True)
-    token = as_column(tokens[...].astype(F32)).astype(jnp.int32)
-
-    received(6, lrecv.at[:, :, pl.ds(0, cut)])
-    received(8, lrecv.at[:, :, pl.ds(cut, VL + 128 - cut)])
-    logits = jnp.sum(lrecv[:, :, 0:VL].astype(F32), axis=0)
-    tail = jnp.sum(lrecv[:, :, VL : VL + 128].astype(F32), axis=0)
+
+    for part in range(3):
+        block = total_z.at[pl.ds(0, 3), :, pl.ds(640 * part, 640)]
+        sum_copy(4 + part, block, block, partner).wait_recv()
+    along_z.wait_recv()
+    rest = mine + total_x[...].astype(F32)
+    logits = jnp.concatenate([jnp.sum(total_z[...].astype(F32), axis=0), rest[:, 0 : VL - CUT]], axis=1)
+    tail = rest[:, VL - CUT :]
     logits = logits * lax.rsqrt((tail[:, 0:1] + tail[:, 32:33]) / D + EPSILON)
     roll_max = jnp.max(logits, axis=-1, keepdims=True)
     roll_sum = jnp.sum(jnp.exp(logits - roll_max), axis=-1, keepdims=True)
@@ -514,6 +561,13 @@
             device_id=sibling, device_id_type=MESH,
         ).wait_send()
     lm_copy.wait_send()
+    for copy in across:
+        copy.wait_send()
+    along_z.wait_send()
+    sum_copy(3, three, three, partner).wait_send()
+    for part in range(3):
+        block = total_z.at[pl.ds(0, 3), :, pl.ds(640 * part, 640)]
+        sum_copy(4 + part, block, block, partner).wait_send()
     along_y().wait_send()
     for copy in pending:
         copy.wait_send()
@@ -561,8 +615,13 @@
             pltpu.VMEM((CHIPS, SEQS, 384), BF16),
             pltpu.VMEM((SEQS, 384), BF16),
             pltpu.VMEM((CHIPS, SEQS, 384), BF16),
-            pltpu.VMEM((CHIPS, SEQS, VL + 128), BF16),
-            pltpu.VMEM((CHIPS, SEQS, VL + 128), BF16),
+            pltpu.VMEM((2, 4, SEQS, VL + 128), BF16),
+            pltpu.VMEM((4, SEQS, CUT), BF16),
+            pltpu.VMEM((4, SEQS, CUT), BF16),
+            pltpu.VMEM((4, SEQS, CUT), BF16),
+            pltpu.VMEM((4, 2, SEQS, REST), BF16),
+            pltpu.VMEM((SEQS, REST), BF16),
+            pltpu.VMEM((SEQS, REST), BF16),
             pltpu.VMEM((SEQS, 128), F32),
             pltpu.VMEM((CHIPS, SEQS, 128), F32),
             pltpu.VMEM((SEQS, 128), F32),
@@ -592,6 +651,8 @@
             pltpu.SemaphoreType.DMA((5,)),
             pltpu.SemaphoreType.DMA((5,)),
             pltpu.SemaphoreType.DMA((2,)),
+            pltpu.SemaphoreType.DMA((8,)),
+            pltpu.SemaphoreType.DMA((8,)),
         ],
         compiler_params=pltpu.CompilerParams(
             collective_id=0, has_side_effects=True, vmem_limit_bytes=32 * 1024 * 1024

time: 72.3 us -> 70.5 us (0.975)
  Pallas kernels: 71.5 us -> 69.7 us
    pallas_call x1, Pallas kernels: 65.6 us -> 63.8 us  [shards(): pl.pallas_call(kernel, out_shape=tuple((pltpu.VMEM(shape, dtype) for shap...]
where the time goes in v3:
time: 70.5 us; the launch traced here: 70.4 us
  Pallas kernels  69.7 us (99%)
    pallas_call x1, Pallas kernels, shards(): pl.pallas_call(kernel, out_shape=tuple((pltpu.VMEM(shape, dtype) for shap...  63.8 us
    pallas_call x1, Pallas kernels, shards(): pl.pallas_call(write_out, out_shape=tuple((jax.ShapeDtypeStruct(shape, dt...  5.9 us

profile of v3, /device:TPU:1, one launch (start us, length us, event | category | flops | bytes accessed | tf_op | source)
XLA Modules:
  0.0 70.4 jit_solution(3451136794089767294)
XLA Ops:
  0.6 63.8 %shard_map.269 = (f32[16,640,128]{2,1,0:T(8,128)S(1)}, f32[1,16]{1,0:T(1,128)S(1)}, f32[1,16]{1,0:T(1,128)S(1)}, bf16[2560,640]{1,0:T(8,128)(2,1)S(1)}, bf16[256...) custom-call(bf16[16,2560]{1,0:T(8,128)(2,1)} %hidden_in.1, ...), custom_call_target="tpu_custom_call" | custom-call | tf_op jit(solution)/shard_map/pallas_call | solution.py:598
  64.5 5.9 %shard_map.270 = (f32[16,640,128]{2,1,0:T(8,128)}, f32[1,16]{1,0:T(1,128)}, f32[1,16]{1,0:T(1,128)}, bf16[2560,640]{1,0:T(8,128)(2,1)}, bf16[2560,640]{1,0:T(8,1...) custom-call(f32[16,640,128]{2,1,0:T(8,128)S(1)} %get-tuple-element.24.refs_0_, ...), custom_call_target="tpu_custom_call" | custom-call | tf_op jit(solution)/shard_map/pallas_call | solution.py:667

commit v4 on v3

--- a/solution.py
+++ b/solution.py
@@ -50,12 +50,6 @@
     r = lax.broadcasted_iota(jnp.int32, (SEQS, SEQS), 0)
     c = lax.broadcasted_iota(jnp.int32, (SEQS, SEQS), 1)
     return jnp.sum(jnp.where(r == c, jnp.broadcast_to(row, (SEQS, SEQS)), 0.0), axis=1, keepdims=True)
-
-
-def as_row(column):
-    r = lax.broadcasted_iota(jnp.int32, (SEQS, 128), 0)
-    c = lax.broadcasted_iota(jnp.int32, (SEQS, 128), 1)
-    return jnp.sum(jnp.where(r == c, jnp.broadcast_to(column, (SEQS, 128)), 0.0), axis=0, keepdims=True)
 
 
 def two_parts(values, width):
@@ -395,6 +389,8 @@
     arrived("OL", 1, 0)
     ici("OL", 1, 0, "-")
     ici("OL", 0, 0, "z")
+    arrived("OH", 0, 1)
+    ici("OH", 0, 1, "-")
     arrived("OL", 3, 0)
     arrived("X", 0, 1)
     arrived("X", 3, 1)
@@ -473,14 +469,15 @@
     mine = jnp.sum(xrecv[:, zl].astype(F32), axis=0)
     pair_sums(2)
 
-    arrived("OH", 0, 1)
-    ici("OH", 0, 1, "+-")
+    ici("OH", 0, 1, "+")
+    arrived("OH", 1, 1)
+    ici("OH", 1, 1, "-")
+    arrived("OH", 3, 0)
+    ici("OH", 3, 0, "+")
     arrived("X", 2, 0)
     ici("X", 2, 0, "z")
     ici("OL", 1, 0, "z")
     ici("OL", 3, 0, "z")
-    arrived("OH", 3, 0)
-    ici("OH", 3, 0, "+")
     arrived("OL", 2, 0)
     ici("OL", 2, 0, "z")
     arrived("BC", 2, 0)
@@ -494,6 +491,11 @@
     arrived("Z", 2, 1)
 
 
+    pltpu.make_async_remote_copy(
+        src_ref=several("d", 7), dst_ref=several("d", 7), send_sem=d2_s.at[ARRAYS.index("d")],
+        recv_sem=d2_r.at[ARRAYS.index("d")], device_id=sibling, device_id_type=MESH,
+    ).wait_recv()
+    dt_out[...] = jnp.concatenate([dts[device].astype(F32) for device in range(2 * CHIPS)], axis=1).astype(BF16)
     for part in range(3):
         block = total_z.at[pl.ds(0, 3), :, pl.ds(640 * part, 640)]
         sum_copy(4 + part, block, block, partner).wait_recv()
@@ -511,7 +513,7 @@
     packed = jnp.zeros((SEQS, 128), F32)
     for at, value in enumerate((roll_max, roll_sum, ref_max, ref_sum, cross, picked)):
         packed = jnp.where(lane == at, jnp.broadcast_to(value, (SEQS, 128)), packed)
-    ssend[...] = packed
+    ssend[...] = jnp.transpose(jnp.concatenate([packed, jnp.zeros((128 - SEQS, 128), F32)], axis=0))[0:8]
 
     to_heads(7, lambda j: ssend, srecv)
     srecv[h] = ssend[...]
@@ -522,27 +524,29 @@
             if (dx, dz) != (0, 0):
                 block = shard_of("b", ((((x + dx) % 4) * 2 + (zl + dz) % 2) * 2 + c))
                 on_chip(block, "b", d2_r.at[ARRAYS.index("b")])
-    arrived("OH", 1, 1)
-    ici("OH", 1, 1, "-")
     arrived("OL", 0, 1)
     arrived("X", 2, 1)
     arrived("OH", 3, 1)
+    arrived("OL", 3, 1)
+    arrived("OL", 1, 1)
+    arrived("OH", 2, 0)
+    arrived("OH", 2, 1)
+    arrived("OL", 2, 1)
 
     received(7, srecv)
-    every = srecv[...]
-    m_all, s_all, rm_all, rs_all, x_all, p_all = (every[:, :, at : at + 1] for at in range(6))
-    roll_top = jnp.max(m_all, axis=0)
-    roll_total = jnp.sum(s_all * jnp.exp(m_all - roll_top[None]), axis=0)
-    ref_top = jnp.max(rm_all, axis=0)
-    ref_scale = jnp.exp(rm_all - ref_top[None])
-    ref_total = jnp.sum(rs_all * ref_scale, axis=0)
-    cross_total = jnp.sum(x_all * ref_scale, axis=0)
+    m_all, s_all, rm_all, rs_all, x_all, p_all = (srecv[:, at, :] for at in range(6))
+    roll_top = jnp.max(m_all, axis=0, keepdims=True)
+    roll_total = jnp.sum(s_all * jnp.exp(m_all - roll_top), axis=0, keepdims=True)
+    ref_top = jnp.max(rm_all, axis=0, keepdims=True)
+    ref_scale = jnp.exp(rm_all - ref_top)
+    ref_total = jnp.sum(rs_all * ref_scale, axis=0, keepdims=True)
+    cross_total = jnp.sum(x_all * ref_scale, axis=0, keepdims=True)
     lse_roll = roll_top + jnp.log(roll_total)
     lse_ref = ref_top + jnp.log(ref_total)
     divergence = cross_total / ref_total - lse_ref + lse_roll
-    logprob = jnp.sum(p_all, axis=0) - lse_roll
-    div_out[...] = as_row(divergence)[:, 0:SEQS]
-    logprob_out[...] = as_row(logprob)[:, 0:SEQS]
+    logprob = jnp.sum(p_all, axis=0, keepdims=True) - lse_roll
+    div_out[...] = divergence[:, 0:SEQS]
+    logprob_out[...] = logprob[:, 0:SEQS]
 
     for piece in PIECES:
         for dz in range(2):
@@ -550,11 +554,14 @@
                 if (dx, dz) != (0, 0) and (piece, dx, dz) not in waited:
                     arrived(piece, dx, dz)
     for at, name in enumerate(ARRAYS):
-        pltpu.make_async_remote_copy(
-            src_ref=bg.at[pl.ds(0, 280)] if name == "b" else several(name, 7), dst_ref=several(name, 7),
-            send_sem=ag_s.at[at], recv_sem=d2_r.at[at], device_id=sibling, device_id_type=MESH,
-        ).wait()
-    dt_out[...] = jnp.concatenate([dts[device].astype(F32) for device in range(2 * CHIPS)], axis=1).astype(BF16)
+        sent = bg.at[pl.ds(0, 280)] if name == "b" else several(name, 7)
+        copy = pltpu.make_async_remote_copy(
+            src_ref=sent, dst_ref=several(name, 7), send_sem=ag_s.at[at], recv_sem=d2_r.at[at], device_id=sibling,
+            device_id_type=MESH,
+        )
+        copy.wait_send()
+        if name != "d":
+            copy.wait_recv()
     for at, name in enumerate(ARRAYS):
         pltpu.make_async_remote_copy(
             src_ref=several(name, 8), dst_ref=several(name, 8), send_sem=d2_s.at[at], recv_sem=d2_r.at[at],
@@ -622,8 +629,8 @@
             pltpu.VMEM((4, 2, SEQS, REST), BF16),
             pltpu.VMEM((SEQS, REST), BF16),
             pltpu.VMEM((SEQS, REST), BF16),
-            pltpu.VMEM((SEQS, 128), F32),
-            pltpu.VMEM((CHIPS, SEQS, 128), F32),
+            pltpu.VMEM((8, 128), F32),
+            pltpu.VMEM((CHIPS, 8, 128), F32),
             pltpu.VMEM((SEQS, 128), F32),
             pltpu.VMEM((SEQS, N), F32),
             pltpu.VMEM((DI, 128), F32),

time: 70.5 us -> 69.6 us (0.987)
  Pallas kernels: 69.7 us -> 68.8 us
    pallas_call x1, Pallas kernels: 63.8 us -> 62.9 us  [shards(): pl.pallas_call(kernel, out_shape=tuple((pltpu.VMEM(shape, dtype) for shap...]
where the time goes in v4:
time: 69.6 us; the launch traced here: 69.5 us
  Pallas kernels  68.8 us (99%)
    pallas_call x1, Pallas kernels, shards(): pl.pallas_call(kernel, out_shape=tuple((pltpu.VMEM(shape, dtype) for shap...  62.9 us
    pallas_call x1, Pallas kernels, shards(): pl.pallas_call(write_out, out_shape=tuple((jax.ShapeDtypeStruct(shape, dt...  5.9 us

profile of v4, /device:TPU:1, one launch (start us, length us, event | category | flops | bytes accessed | tf_op | source)
XLA Modules:
  0.0 69.5 jit_solution(6244045425294078152)
XLA Ops:
  0.6 62.9 %shard_map.269 = (f32[16,640,128]{2,1,0:T(8,128)S(1)}, f32[1,16]{1,0:T(1,128)S(1)}, f32[1,16]{1,0:T(1,128)S(1)}, bf16[2560,640]{1,0:T(8,128)(2,1)S(1)}, bf16[256...) custom-call(bf16[16,2560]{1,0:T(8,128)(2,1)} %hidden_in.1, ...), custom_call_target="tpu_custom_call" | custom-call | tf_op jit(solution)/shard_map/pallas_call | solution.py:605
  63.6 5.9 %shard_map.270 = (f32[16,640,128]{2,1,0:T(8,128)}, f32[1,16]{1,0:T(1,128)}, f32[1,16]{1,0:T(1,128)}, bf16[2560,640]{1,0:T(8,128)(2,1)}, bf16[2560,640]{1,0:T(8,1...) custom-call(f32[16,640,128]{2,1,0:T(8,128)S(1)} %get-tuple-element.24.refs_0_, ...), custom_call_target="tpu_custom_call" | custom-call | tf_op jit(solution)/shard_map/pallas_call | solution.py:674

commit v5 on v4

--- a/solution.py
+++ b/solution.py
@@ -332,9 +332,7 @@
     gate = jnp.sum(precv[:, :, 1024:1664].astype(F32), axis=0) * scale_in
     ssm_out = y_acc[...] + per_head(skip_gain[...]) * x_conv
     gated = ssm_out * silu(gate)
-    squares = jnp.sum(gated * gated, axis=-1, keepdims=True)
-    gsend[:, 0:640] = (gated * short_rows[1:2, :]).astype(BF16)
-    gsend[:, 640:768] = two_parts(squares, 64)
+    gsend[...] = gated.astype(BF16)
 
     to_chips(3, lambda j: gsend, grecv)
     grecv[k] = gsend[...]
@@ -348,12 +346,12 @@
 
     sibling_own("o")
     received(3, grecv)
+    values = grecv[...].astype(F32).reshape(CHIPS * SEQS, DI)
     mixed = lax.dot_general(
-        grecv[:, :, 0:640].reshape(CHIPS * SEQS, 640), og[slice_rows, :], (((1,), (1,)), ((), ())),
+        (values * short_rows[1:2, :]).astype(BF16), og[slice_rows, :], (((1,), (1,)), ((), ())),
         preferred_element_type=F32,
     )
-    parts = grecv[:, :, 640:768].astype(F32)
-    sq = (parts[:, :, 0:1] + parts[:, :, 64:65]).reshape(CHIPS * SEQS, 1)
+    sq = jnp.sum(values * values, axis=-1, keepdims=True)
     rsend[:, :, 0:SLICE] = mixed.astype(BF16).reshape(CHIPS, SEQS, SLICE)
     rsend[:, :, SLICE:384] = two_parts(sq, 32).reshape(CHIPS, SEQS, 64)
     to_heads(4, lambda j: rsend.at[j], rrecv)
@@ -616,8 +614,8 @@
             pltpu.VMEM((2, CHIPS, 1, SLICE), F32),
             pltpu.VMEM((CHIPS, SEQS, 1664), BF16),
             pltpu.VMEM((CHIPS, SEQS, 1664), BF16),
-            pltpu.VMEM((SEQS, 768), BF16),
-            pltpu.VMEM((CHIPS, SEQS, 768), BF16),
+            pltpu.VMEM((SEQS, DI), BF16),
+            pltpu.VMEM((CHIPS, SEQS, DI), BF16),
             pltpu.VMEM((CHIPS, SEQS, 384), BF16),
             pltpu.VMEM((CHIPS, SEQS, 384), BF16),
             pltpu.VMEM((SEQS, 384), BF16),

time: 69.6 us -> 69.2 us (level)
  no operation moved by 1% of the time
where the time goes in v5:
time: 69.2 us; the launch traced here: 69.1 us
  Pallas kernels  68.5 us (99%)
    pallas_call x1, Pallas kernels, shards(): pl.pallas_call(kernel, out_shape=tuple((pltpu.VMEM(shape, dtype) for shap...  62.6 us
    pallas_call x1, Pallas kernels, shards(): pl.pallas_call(write_out, out_shape=tuple((jax.ShapeDtypeStruct(shape, dt...  5.9 us

profile of v5, /device:TPU:1, one launch (start us, length us, event | category | flops | bytes accessed | tf_op | source)
XLA Modules:
  0.0 69.1 jit_solution(11061771910968384290)
XLA Ops:
  0.6 62.6 %shard_map.269 = (f32[16,640,128]{2,1,0:T(8,128)S(1)}, f32[1,16]{1,0:T(1,128)S(1)}, f32[1,16]{1,0:T(1,128)S(1)}, bf16[2560,640]{1,0:T(8,128)(2,1)S(1)}, bf16[256...) custom-call(bf16[16,2560]{1,0:T(8,128)(2,1)} %hidden_in.1, ...), custom_call_target="tpu_custom_call" | custom-call | tf_op jit(solution)/shard_map/pallas_call | solution.py:603
  63.2 5.9 %shard_map.270 = (f32[16,640,128]{2,1,0:T(8,128)}, f32[1,16]{1,0:T(1,128)}, f32[1,16]{1,0:T(1,128)}, bf16[2560,640]{1,0:T(8,128)(2,1)}, bf16[2560,640]{1,0:T(8,1...) custom-call(f32[16,640,128]{2,1,0:T(8,128)S(1)} %get-tuple-element.24.refs_0_, ...), custom_call_target="tpu_custom_call" | custom-call | tf_op jit(solution)/shard_map/pallas_call | solution.py:672
